TPU v7x, 32 devices: a whole 2x2x4 slice. The times are simulated.
32 devices in a mesh: cfg: 4 (over x, y), sp: 8 (over z, core).
Axes of the slice: x: 2, y: 2, z: 4, core: 2. Of those that a mesh axis runs over, the one named last changes fastest.
Arguments:
- x_txt: bfloat16 [2048, 3072], P(('cfg', 'sp')), parts along dimension 0
- x_img: bfloat16 [16384, 3072], P(('cfg', 'sp')), parts along dimension 0
- cond_vec: bfloat16 [4, 3072], P('cfg'), parts along dimension 0
- cos_img: float32 [4096, 64], P('sp')
- sin_img: float32 [4096, 64], P('sp')
- z_lat: float32 [16384, 64], P(('cfg', 'sp')), parts along dimension 0
- t_cur: float32 [1], replicated
- t_next: float32 [1], replicated
- w_mod: bfloat16 [2, 3072, 9216], replicated
- b_mod: bfloat16 [2, 9216], replicated
- w_in: bfloat16 [2, 3072, 21504], replicated
- b_in: bfloat16 [2, 21504], replicated
- qk_gain: bfloat16 [2, 2, 128], replicated
- w_out: bfloat16 [2, 15360, 3072], replicated
- b_out: bfloat16 [2, 3072], replicated
- w_fmod: bfloat16 [3072, 6144], replicated
- b_fmod: bfloat16 [6144], replicated
- w_final: bfloat16 [3072, 64], replicated
- b_final: bfloat16 [64], replicated
Outputs:
- output: float32 [16384, 64], P(('cfg', 'sp')), parts along dimension 0
There are 4 independent parts. A program takes and returns all parts, laid end to end along the dimension named above; an argument that names none is the same for every part.
All inputs are finite; a program needn't handle non-finite values.
Results may differ from a plain program's by a relative error of at most 0.00454191.
Values are sent between devices in bfloat16 or wider.
A program may use at most 2.5 GiB of HBM per device.

v0:
```python
import jax
import jax.numpy as jnp
from jax import lax
from jax.sharding import PartitionSpec as P, NamedSharding

EPS = 1e-6


def layer_norm(x_rows):
    x_f32 = x_rows.astype(jnp.float32)
    centered = x_f32 - jnp.mean(x_f32, axis=-1, keepdims=True)
    return centered * lax.rsqrt(jnp.mean(centered * centered, axis=-1, keepdims=True) + EPS)


def head_norm(head_vals, gain_vec):
    vals_f32 = head_vals.astype(jnp.float32)
    return vals_f32 * lax.rsqrt(jnp.mean(vals_f32 * vals_f32, axis=-1, keepdims=True) + EPS) * gain_vec.astype(jnp.float32)


def rotate(head_vals, cos_tab, sin_tab):
    half_dim = head_vals.shape[-1] // 2
    lead_half = head_vals[..., :half_dim]
    tail_half = head_vals[..., half_dim:]
    cos_b = cos_tab[:, None, :]
    sin_b = sin_tab[:, None, :]
    return jnp.concatenate([lead_half * cos_b - tail_half * sin_b, lead_half * sin_b + tail_half * cos_b], axis=-1)


def query_block(q_count):
    for block_size in (512, 256, 128, 64, 32, 16, 8):
        if q_count % block_size == 0:
            return block_size
    return q_count


def local_attention(q_all, k_all, v_all):
    q_count, n_heads, head_dim = q_all.shape
    block_size = query_block(q_count)
    score_scale = head_dim ** -0.5

    def per_block(q_block):
        scores = jnp.einsum('qhd,khd->hqk', q_block, k_all, preferred_element_type=jnp.float32) * score_scale
        probs = jnp.exp(scores - jnp.max(scores, axis=-1, keepdims=True))
        row_sum = jnp.sum(probs, axis=-1)
        weighted = jnp.einsum('hqk,khd->qhd', probs.astype(jnp.bfloat16), v_all, preferred_element_type=jnp.float32)
        return (weighted / jnp.transpose(row_sum)[:, :, None]).astype(jnp.bfloat16)

    attended = lax.map(per_block, q_all.reshape(q_count // block_size, block_size, n_heads, head_dim))
    return attended.reshape(q_count, n_heads, head_dim)


def exchange_attention(q_heads, k_heads, v_heads):
    q_all = lax.all_to_all(q_heads, 'sp', 1, 0, tiled=True)
    k_all = lax.all_to_all(k_heads, 'sp', 1, 0, tiled=True)
    v_all = lax.all_to_all(v_heads, 'sp', 1, 0, tiled=True)
    attended = local_attention(q_all, k_all, v_all)
    return lax.all_to_all(attended, 'sp', 0, 1, tiled=True)


def single_block(x_loc, n_txt, mod_in, cos_loc, sin_loc, weights, is_last):
    w_mod, b_mod, w_in, b_in, qk_gain, w_out, b_out = weights
    d_model = x_loc.shape[-1]
    head_dim = qk_gain.shape[-1]
    n_heads = d_model // head_dim
    mod_vals = jnp.dot(mod_in, w_mod, preferred_element_type=jnp.float32) + b_mod.astype(jnp.float32)
    shift_m = mod_vals[:, :d_model]
    scale_m = mod_vals[:, d_model:2 * d_model]
    gate_m = mod_vals[:, 2 * d_model:]
    normed = (layer_norm(x_loc) * (1.0 + scale_m) + shift_m).astype(jnp.bfloat16)
    if is_last:
        txt_kv = (jnp.dot(normed[:n_txt], w_in[:, d_model:3 * d_model], preferred_element_type=jnp.float32) + b_in[d_model:3 * d_model].astype(jnp.float32)).astype(jnp.bfloat16)
        img_proj = (jnp.dot(normed[n_txt:], w_in, preferred_element_type=jnp.float32) + b_in.astype(jnp.float32)).astype(jnp.bfloat16)
        q_rows = img_proj[:, :d_model]
        k_rows = jnp.concatenate([txt_kv[:, :d_model], img_proj[:, d_model:2 * d_model]], axis=0)
        v_rows = jnp.concatenate([txt_kv[:, d_model:], img_proj[:, 2 * d_model:3 * d_model]], axis=0)
        u_rows = img_proj[:, 3 * d_model:]
        residual = x_loc[n_txt:]
        q_cos = cos_loc[n_txt:]
        q_sin = sin_loc[n_txt:]
    else:
        proj_rows = (jnp.dot(normed, w_in, preferred_element_type=jnp.float32) + b_in.astype(jnp.float32)).astype(jnp.bfloat16)
        q_rows = proj_rows[:, :d_model]
        k_rows = proj_rows[:, d_model:2 * d_model]
        v_rows = proj_rows[:, 2 * d_model:3 * d_model]
        u_rows = proj_rows[:, 3 * d_model:]
        residual = x_loc
        q_cos = cos_loc
        q_sin = sin_loc
    q_heads = rotate(head_norm(q_rows.reshape(-1, n_heads, head_dim), qk_gain[0]), q_cos, q_sin).astype(jnp.bfloat16)
    k_heads = rotate(head_norm(k_rows.reshape(-1, n_heads, head_dim), qk_gain[1]), cos_loc, sin_loc).astype(jnp.bfloat16)
    v_heads = v_rows.reshape(-1, n_heads, head_dim)
    attended = exchange_attention(q_heads, k_heads, v_heads).reshape(-1, d_model)
    mlp_act = jax.nn.gelu(u_rows.astype(jnp.float32), approximate=True).astype(jnp.bfloat16)
    update = jnp.dot(attended, w_out[:d_model], preferred_element_type=jnp.float32) + jnp.dot(mlp_act, w_out[d_model:], preferred_element_type=jnp.float32) + b_out.astype(jnp.float32)
    return (residual.astype(jnp.float32) + gate_m * update).astype(jnp.bfloat16)


def solution(mesh):
    token_spec = P(('cfg', 'sp'), None)
    in_specs = (token_spec, token_spec, P('cfg', None), P('sp', None), P('sp', None), token_spec) + (P(),) * 13

    def body(x_txt, x_img, cond_vec, cos_img, sin_img, z_lat, t_cur, t_next, w_mod, b_mod, w_in, b_in, qk_gain, w_out, b_out, w_fmod, b_fmod, w_final, b_final):
        n_txt = x_txt.shape[0]
        d_model = x_txt.shape[1]
        half_dim = cos_img.shape[1]
        mod_in = jax.nn.silu(cond_vec.astype(jnp.float32)).astype(jnp.bfloat16)
        cos_loc = jnp.concatenate([jnp.ones((n_txt, half_dim), jnp.float32), cos_img], axis=0)
        sin_loc = jnp.concatenate([jnp.zeros((n_txt, half_dim), jnp.float32), sin_img], axis=0)
        x_loc = jnp.concatenate([x_txt, x_img], axis=0)
        n_layers = w_mod.shape[0]
        for layer_idx in range(n_layers):
            weights = (w_mod[layer_idx], b_mod[layer_idx], w_in[layer_idx], b_in[layer_idx], qk_gain[layer_idx], w_out[layer_idx], b_out[layer_idx])
            x_loc = single_block(x_loc, n_txt, mod_in, cos_loc, sin_loc, weights, layer_idx == n_layers - 1)
        fmod_vals = jnp.dot(mod_in, w_fmod, preferred_element_type=jnp.float32) + b_fmod.astype(jnp.float32)
        final_in = (layer_norm(x_loc) * (1.0 + fmod_vals[:, d_model:]) + fmod_vals[:, :d_model]).astype(jnp.bfloat16)
        velocity = jnp.dot(final_in, w_final, preferred_element_type=jnp.float32) + b_final.astype(jnp.float32)
        return z_lat + (t_next - t_cur) * velocity

    return jax.shard_map(body, mesh=mesh, in_specs=in_specs, out_specs=token_spec, check_vma=False)
```

profile of v0, /device:TPU:0, one launch (start us, length us, event | category | flops | bytes accessed | tf_op | source)
XLA Modules:
  0.0 1780.3 jit_solution(6751456755082499991)
XLA Ops:
  1.5 20.7 %fusion.59 = f32[1,9216]{1,0:T(1,128)} fusion(bf16[2,3072,9216]{2,1,0:T(8,128)(2,1)} %param.31, bf16[1,3072]{1,0:T(2,128)(2,1)} %param.25), kind=kOutput, calls=%fused_computation.42 | convolution fusion | flops 56641536 | bytes 56672256 | tf_op jit(solution)/shard_map/dot_general | solution.py:65
  29.1 89.4 %add_convert_fusion = bf16[576,21504]{1,0:T(8,128)(2,1)} fusion(bf16[2,3072,21504]{2,1,0:T(8,128)(2,1)} %param.33, f32[21504]{0:T(1024)S(1)} %bitcast.265, f32[3072]{0:T(1024)S(1)} %bitcast.271, f32[3072]{0:T(1024)S(1)} %bitcast.272, f32[576]{0:T(1024)S(1)} %add_rsqrt_fusion.5, f32[576]{0:T(1024)S(1)} %broadcast_multiply_fusion.1, ...), kind=kOutput, calls=%fused_computation.50 | convolution fusion | flops 76142149632 | bytes 160547328 | tf_op jit(solution)/shard_map/dot_general | solution.py:81
  172.9 72.8 %all-to-all-done.1 = bf16[576,24,128]{2,0,1:T(8,128)(2,1)} async-done(((bf16[576,24,128]{2,0,1:T(8,128)(2,1)}), bf16[576,24,128]{2,0,1:T(8,128)(2,1)}, u32[]{:S(2)}, u32[]{:S(2)}) %all-to-all-start.1) | async-done | bytes 3538976 | tf_op jit(solution)/shard_map/all_to_all | solution.py:54
  255.0 74.9 %all-to-all-done = bf16[576,24,128]{2,0,1:T(8,128)(2,1)} async-done(((bf16[576,24,128]{2,0,1:T(8,128)(2,1)}), bf16[576,24,128]{2,0,1:T(8,128)(2,1)}, u32[]{:S(2)}, u32[]{:S(2)}) %all-to-all-start) | async-done | bytes 3538976 | tf_op jit(solution)/shard_map/all_to_all | solution.py:53
  334.4 85.9 %slice_bitcast_fusion = bf16[3072,21504]{1,0:T(8,128)(2,1)} fusion(bf16[2,3072,21504]{2,1,0:T(8,128)(2,1)} %param.33), kind=kLoop, calls=%fused_computation.32 | loop fusion | bytes 264241152 | tf_op jit(solution)/shard_map/squeeze | solution.py:112
  420.4 19.9 %fusion.57 = f32[1,9216]{1,0:T(1,128)S(1)} fusion(bf16[2,3072,9216]{2,1,0:T(8,128)(2,1)} %param.31, bf16[1,3072]{1,0:T(2,128)(2,1)S(1)} %copy-done.16), kind=kOutput, calls=%fused_computation.40 | convolution fusion | flops 56641536 | bytes 56666112 | tf_op jit(solution)/shard_map/dot_general | solution.py:65
  455.1 367.7 %while.20 = (s32[]{:T(128)}, bf16[9,512,3,128]{3,1,0,2:T(8,128)(2,1)}, bf16[9,512,3,128]{3,1,0,2:T(8,128)(2,1)}, bf16[4608,3,128]{2,0,1:T(8,128)(2,1)}, bf16[4608,3,128]{2,0,1:T(8,128)(2,1)}, /*index=5*/s32[]{:T(128)}) while((s32[]{:T(128)}, bf16[9,512,3,128]{3,1,0,2:T(8,128)(2,1)}, bf16[9,512,3,128]{3,1,0,2:T(8,128)(2,1)}, ...), condition=%wide.region_7.8_spmd, body=%wide.region_4.7_spmd.sunk | while | flops 3680891904 | bytes 106986592 | solution.py:48
  455.1 15.3 multiply_reduce_fusion.8
  470.4 12.9 fusion.205
  495.9 15.3 multiply_reduce_fusion.8
  511.2 12.9 fusion.205
  536.8 15.3 multiply_reduce_fusion.8
  552.1 12.9 fusion.205
  565.0 12.6 fusion.206
  577.6 15.3 multiply_reduce_fusion.8
  592.9 12.9 fusion.205
  618.5 15.3 multiply_reduce_fusion.8
  633.8 12.9 fusion.205
  646.7 12.6 fusion.206
  659.3 15.3 multiply_reduce_fusion.8
  674.7 12.9 fusion.205
  700.2 15.3 multiply_reduce_fusion.8
  715.5 12.9 fusion.205
  728.4 12.6 fusion.206
  741.0 15.3 multiply_reduce_fusion.8
  756.4 12.9 fusion.205
  769.3 12.6 fusion.206
  781.9 15.3 multiply_reduce_fusion.8
  797.2 12.9 fusion.205
  810.1 12.6 fusion.206
  822.8 18.3 %copy.154 = bf16[4608,3,128]{2,1,0:T(4,128)(2,1)} copy(bf16[4608,3,128]{2,0,1:T(8,128)(2,1)} %bitcast.29) | data formatting | bytes 7077888 | tf_op jit(solution)/shard_map/reshape | solution.py:49
  846.1 55.4 %fusion.53 = f32[576,3072]{1,0:T(8,128)} fusion(bf16[2,15360,3072]{2,1,0:T(8,128)(2,1)} %param.36, bf16[576,21504]{1,0:T(8,128)(2,1)} %add_convert_fusion), kind=kOutput, calls=%fused_computation.36 | convolution fusion | flops 43557322752 | bytes 96731136 | tf_op jit(solution)/shard_map/dot_general | solution.py:94
  901.5 49.6 %all-to-all-done.3 = bf16[4608,3,128]{2,1,0:T(4,128)(2,1)} async-done(((bf16[4608,3,128]{2,1,0:T(4,128)(2,1)}), bf16[4608,3,128]{2,1,0:T(4,128)(2,1)}, u32[]{:S(2)}, u32[]{:S(2)}) %all-to-all-start.3) | async-done | bytes 3538976 | tf_op jit(solution)/shard_map/all_to_all | solution.py:57
  959.4 19.1 %convert_reduce_fusion.1 = (f32[576]{0:T(1024)S(1)}, bf16[576,3072]{1,0:T(8,128)(2,1)S(1)}) fusion(f32[3072]{0:T(1024)S(1)} %bitcast.276, f32[576,3072]{1,0:T(8,128)} %fusion.53, bf16[576,3072]{0,1:T(8,128)(2,1)} %bitcast.250, bf16[2,15360,3072]{2,1,0:T(8,128)(2,1)} %param.36, f32[3072]{0:T(1024)S(1)} %bitcast.270, bf16[512,3072]{1,0:T(8,128)(2,1)} %param.24, ...), kind=kOutput, calls=%fused_computation.96 | convolution fusion | flops 10891099136 | bytes 36989184 | tf_op jit(solution)/shard_map/dot_general | solution.py:94
  984.1 15.6 fusion.118
  1000.7 82.4 %add_convert_fusion.1 = bf16[512,21504]{1,0:T(8,128)(2,1)} fusion(f32[21504]{0:T(1024)S(1)} %bitcast.264, bf16[576,3072]{1,0:T(8,128)(2,1)} %fusion.110, bf16[2,3072,21504]{2,1,0:T(8,128)(2,1)} %param.33), kind=kOutput, calls=%fused_computation.55 | convolution fusion | flops 67667755008 | bytes 157372416 | tf_op jit(solution)/shard_map/dot_general | solution.py:72
  1118.1 59.9 %all-to-all-done.6 = bf16[576,24,128]{2,0,1:T(8,128)(2,1)} async-done(((bf16[576,24,128]{2,0,1:T(8,128)(2,1)}), bf16[576,24,128]{2,0,1:T(8,128)(2,1)}, u32[]{:S(2)}, u32[]{:S(2)}) %all-to-all-start.6) | async-done | bytes 3538976 | tf_op jit(solution)/shard_map/all_to_all | solution.py:55
  1199.0 63.4 %all-to-all-done.5 = bf16[576,24,128]{2,0,1:T(8,128)(2,1)} async-done(((bf16[576,24,128]{2,0,1:T(8,128)(2,1)}), bf16[576,24,128]{2,0,1:T(8,128)(2,1)}, u32[]{:S(2)}, u32[]{:S(2)}) %all-to-all-start.5) | async-done | bytes 3538976 | tf_op jit(solution)/shard_map/all_to_all | solution.py:54
  1268.4 14.3 fusion.148
  1291.4 46.3 %all-to-all-done.4 = bf16[512,24,128]{2,0,1:T(8,128)(2,1)S(1)} async-done(((bf16[512,24,128]{2,0,1:T(8,128)(2,1)}), bf16[512,24,128]{2,0,1:T(8,128)(2,1)S(1)}, u32[]{:S(2)}, u32[]{:S(2)}) %all-to-all-start.4) | async-done | bytes 3145760 | tf_op jit(solution)/shard_map/all_to_all | solution.py:53
  1337.8 311.0 %while.21 = (s32[]{:T(128)}, bf16[8,512,3,128]{3,1,0,2:T(8,128)(2,1)}, bf16[8,512,3,128]{3,1,2,0:T(8,128)(2,1)S(1)}, bf16[4608,3,128]{2,0,1:T(8,128)(2,1)}, bf16[4608,3,128]{2,0,1:T(8,128)(2,1)}, /*index=5*/s32[]{:T(128)}) while((s32[]{:T(128)}, bf16[8,512,3,128]{3,1,0,2:T(8,128)(2,1)}, bf16[8,512,3,128]{3,1,2,0:T(8,128)(2,1)S(1)}, ...), condition=%wide.region_15.16_spmd, body=%wide.region_12.15_spmd.sunk | while | flops 3680891904 | bytes 106986088 | solution.py:48
  1337.8 13.3 multiply_reduce_fusion.9
  1351.1 12.9 fusion.210
  1364.0 12.6 fusion.211
  1376.7 13.3 multiply_reduce_fusion.9
  1390.0 12.9 fusion.210
  1415.5 13.3 multiply_reduce_fusion.9
  1428.9 12.9 fusion.210
  1441.8 12.6 fusion.211
  1454.4 13.3 multiply_reduce_fusion.9
  1467.7 12.9 fusion.210
  1493.3 13.3 multiply_reduce_fusion.9
  1506.6 12.9 fusion.210
  1519.5 12.6 fusion.211
  1532.2 13.3 multiply_reduce_fusion.9
  1545.5 12.9 fusion.210
  1571.0 13.3 multiply_reduce_fusion.9
  1584.4 12.9 fusion.210
  1597.3 12.6 fusion.211
  1609.9 13.3 multiply_reduce_fusion.9
  1623.3 12.9 fusion.210
  1660.3 50.0 %fusion.51 = f32[512,3072]{1,0:T(8,128)} fusion(bf16[2,15360,3072]{2,1,0:T(8,128)(2,1)} %param.36, bf16[512,21504]{1,0:T(8,128)(2,1)} %add_convert_fusion.1), kind=kOutput, calls=%fused_computation.34 | convolution fusion | flops 38717620224 | bytes 94371840 | tf_op jit(solution)/shard_map/dot_general | solution.py:94
  1710.3 43.7 %all-to-all-done.7 = bf16[4096,3,128]{2,1,0:T(4,128)(2,1)} async-done(((bf16[4096,3,128]{2,1,0:T(4,128)(2,1)}), bf16[4096,3,128]{2,1,0:T(4,128)(2,1)}, u32[]{:S(2)}, u32[]{:S(2)}) %all-to-all-start.7) | async-done | bytes 3145760 | tf_op jit(solution)/shard_map/all_to_all | solution.py:57
  1759.5 17.4 convert_reduce_fusion.2
  (194 shorter events, 301.5 us)
Async XLA Ops:
  0.0 1777.9 %copy-start = (bf16[3072,64]{0,1:T(8,128)(2,1)S(1)}, bf16[3072,64]{0,1:T(8,128)(2,1)}, u32[]{:S(2)}) copy-start(bf16[3072,64]{0,1:T(8,128)(2,1)} %param.40) | copy-start | bytes 1179652
  1.5 23.9 %copy-start.2 = (bf16[512,3072]{1,0:T(8,128)(2,1)S(1)}, bf16[512,3072]{1,0:T(8,128)(2,1)}, u32[]{:S(2)}) copy-start(bf16[512,3072]{1,0:T(8,128)(2,1)} %param.24) | copy-start | bytes 9437188
  22.2 6.8 copy-start.14
  138.8 2.1 copy-start.32
  138.8 2.7 copy-start.19
  138.8 2.8 copy-start.20
  141.7 7.6 copy-start.9
  141.8 7.5 copy-start.11
  141.8 7.4 copy-start.5
  141.9 7.4 copy-start.7
  159.4 86.3 %all-to-all-start.1 = ((bf16[576,24,128]{2,0,1:T(8,128)(2,1)}), bf16[576,24,128]{2,0,1:T(8,128)(2,1)}, u32[]{:S(2)}, u32[]{:S(2)}) async-start(bf16[576,24,128]{2,0,1:T(8,128)(2,1)} %pad_maximum_fusion.2), calls=%async_computation.1 | async-start | bytes 7077888 | tf_op jit(solution)/shard_map/all_to_all | solution.py:54
  245.7 84.2 %all-to-all-start = ((bf16[576,24,128]{2,0,1:T(8,128)(2,1)}), bf16[576,24,128]{2,0,1:T(8,128)(2,1)}, u32[]{:S(2)}, u32[]{:S(2)}) async-start(bf16[576,24,128]{2,0,1:T(8,128)(2,1)} %pad_maximum_fusion.1), calls=%async_computation | async-start | bytes 7077888 | tf_op jit(solution)/shard_map/all_to_all | solution.py:53
  329.9 121.2 %all-to-all-start.2 = ((bf16[576,24,128]{2,0,1:T(8,128)(2,1)}), bf16[576,24,128]{2,0,1:T(8,128)(2,1)}, u32[]{:S(2)}, u32[]{:S(2)}) async-start(bf16[576,24,128]{2,0,1:T(8,128)(2,1)} %bitcast.246), calls=%async_computation.2 | async-start | bytes 7077888 | tf_op jit(solution)/shard_map/all_to_all | solution.py:55
  334.4 85.9 %copy-start.16 = (bf16[1,3072]{1,0:T(2,128)(2,1)S(1)}, bf16[1,3072]{1,0:T(2,128)(2,1)}, u32[]{:S(2)}) copy-start(bf16[1,3072]{1,0:T(2,128)(2,1)} %param.25) | copy-start | bytes 18436
  420.3 19.9 %copy-start.18 = (f32[1,9216]{1,0:T(1,128)S(1)}, f32[1,9216]{1,0:T(1,128)}, u32[]{:S(2)}) copy-start(f32[1,9216]{1,0:T(1,128)} %get-tuple-element.143) | copy-start | bytes 110596
  420.4 20.0 %copy-start.24 = (bf16[2,3072]{1,0:T(2,128)(2,1)S(1)}, bf16[2,3072]{1,0:T(2,128)(2,1)}, u32[]{:S(2)}) copy-start(bf16[2,3072]{1,0:T(2,128)(2,1)} %param.37) | copy-start | bytes 36868
  470.4 12.9 copy-start.4
  511.2 12.9 copy-start.4
  552.1 12.9 copy-start.4
  592.9 12.9 copy-start.4
  633.8 12.9 copy-start.4
  674.6 12.9 copy-start.4
  715.5 12.9 copy-start.4
  756.4 12.9 copy-start.4
  797.2 12.9 copy-start.4
  841.1 110.0 %all-to-all-start.3 = ((bf16[4608,3,128]{2,1,0:T(4,128)(2,1)}), bf16[4608,3,128]{2,1,0:T(4,128)(2,1)}, u32[]{:S(2)}, u32[]{:S(2)}) async-start(bf16[4608,3,128]{2,1,0:T(4,128)(2,1)} %copy.154), calls=%async_computation.3 | async-start | bytes 9437184 | tf_op jit(solution)/shard_map/all_to_all | solution.py:57
  901.5 57.9 %copy-start.15 = (bf16[64,3072]{1,0:T(8,128)(2,1)S(1)}, bf16[64,3072]{1,0:T(8,128)(2,1)}, u32[]{:S(2)}) copy-start(bf16[64,3072]{1,0:T(8,128)(2,1)} %param.23) | copy-start | bytes 1179652
  901.5 57.9 %copy-start.27 = (f32[1,3072]{1,0:T(1,128)S(1)}, f32[1,3072]{1,0:T(1,128)}, u32[]{:S(2)}) copy-start(f32[1,3072]{1,0:T(1,128)} %get-tuple-element.145) | copy-start | bytes 36868
  901.5 57.9 %copy-start.30 = (f32[1,3072]{1,0:T(1,128)S(1)}, f32[1,3072]{1,0:T(1,128)}, u32[]{:S(2)}) copy-start(f32[1,3072]{1,0:T(1,128)} %get-tuple-element.151) | copy-start | bytes 36868
  959.4 20.9 %copy-start.22 = (f32[1,3072]{1,0:T(1,128)S(1)}, f32[1,3072]{1,0:T(1,128)}, u32[]{:S(2)}) copy-start(f32[1,3072]{1,0:T(1,128)} %get-tuple-element.141) | copy-start | bytes 36868
  959.4 20.9 %copy-start.23 = (f32[1,3072]{1,0:T(1,128)S(1)}, f32[1,3072]{1,0:T(1,128)}, u32[]{:S(2)}) copy-start(f32[1,3072]{1,0:T(1,128)} %get-tuple-element.142) | copy-start | bytes 36868
  978.5 1.8 copy-start.1
  978.5 5.6 copy-start.25
  984.1 16.6 copy-start.21
  1083.0 7.8 copy-start.13
  1093.6 84.4 %all-to-all-start.6 = ((bf16[576,24,128]{2,0,1:T(8,128)(2,1)}), bf16[576,24,128]{2,0,1:T(8,128)(2,1)}, u32[]{:S(2)}, u32[]{:S(2)}) async-start(bf16[576,24,128]{2,0,1:T(8,128)(2,1)} %copy_bitcast_fusion), calls=%async_computation.6 | async-start | bytes 7077888 | tf_op jit(solution)/shard_map/all_to_all | solution.py:55
  1104.8 2.1 copy-start.34
  1106.9 4.9 copy-start.6
  1106.9 4.9 copy-start.8
  1178.0 84.4 %all-to-all-start.5 = ((bf16[576,24,128]{2,0,1:T(8,128)(2,1)}), bf16[576,24,128]{2,0,1:T(8,128)(2,1)}, u32[]{:S(2)}, u32[]{:S(2)}) async-start(bf16[576,24,128]{2,0,1:T(8,128)(2,1)} %pad_maximum_fusion.4), calls=%async_computation.5 | async-start | bytes 7077888 | tf_op jit(solution)/shard_map/all_to_all | solution.py:54
  1182.8 6.0 copy-start.33
  1188.6 4.6 copy-start.10
  1188.6 4.6 copy-start.12
  1195.6 72.2 %copy-start.36 = (bf16[64]{0:T(256)(128)(2,1)S(1)}, bf16[64]{0:T(256)(128)(2,1)}, u32[]{:S(2)}) copy-start(bf16[64]{0:T(256)(128)(2,1)} %param.41) | copy-start | bytes 388
  1195.6 72.8 %copy-start.17 = (bf16[1,3072]{1,0:T(2,128)(2,1)S(1)}, bf16[1,3072]{1,0:T(2,128)(2,1)}, u32[]{:S(2)}) copy-start(bf16[1,3072]{1,0:T(2,128)(2,1)} %param.25) | copy-start | bytes 18436
  1262.4 75.4 %all-to-all-start.4 = ((bf16[512,24,128]{2,0,1:T(8,128)(2,1)}), bf16[512,24,128]{2,0,1:T(8,128)(2,1)S(1)}, u32[]{:S(2)}, u32[]{:S(2)}) async-start(bf16[512,24,128]{2,0,1:T(8,128)(2,1)} %pad_maximum_fusion.5), calls=%async_computation.4 | async-start | bytes 6291456 | tf_op jit(solution)/shard_map/all_to_all | solution.py:53
  1268.4 14.3 copy-start.31
  1351.1 12.9 copy-start.3
  1390.0 12.9 copy-start.3
  1428.9 12.9 copy-start.3
  1467.7 12.9 copy-start.3
  1506.6 12.9 copy-start.3
  1545.5 12.9 copy-start.3
  1584.4 12.9 copy-start.3
  1623.3 12.9 copy-start.3
  1655.6 98.4 %all-to-all-start.7 = ((bf16[4096,3,128]{2,1,0:T(4,128)(2,1)}), bf16[4096,3,128]{2,1,0:T(4,128)(2,1)}, u32[]{:S(2)}, u32[]{:S(2)}) async-start(bf16[4096,3,128]{2,1,0:T(4,128)(2,1)} %copy.166), calls=%async_computation.7 | async-start | bytes 8388608 | tf_op jit(solution)/shard_map/all_to_all | solution.py:57
  1710.3 49.2 %copy-start.26 = (f32[1,3072]{1,0:T(1,128)S(1)}, f32[1,3072]{1,0:T(1,128)}, u32[]{:S(2)}) copy-start(f32[1,3072]{1,0:T(1,128)} %get-tuple-element.140) | copy-start | bytes 36868
  1759.5 18.4 %copy-start.28 = (f32[1,3072]{1,0:T(1,128)S(1)}, f32[1,3072]{1,0:T(1,128)}, u32[]{:S(2)}) copy-start(f32[1,3072]{1,0:T(1,128)} %get-tuple-element.148) | copy-start | bytes 36868
  1759.5 18.4 %copy-start.29 = (f32[1,3072]{1,0:T(1,128)S(1)}, f32[1,3072]{1,0:T(1,128)}, u32[]{:S(2)}) copy-start(f32[1,3072]{1,0:T(1,128)} %get-tuple-element.149) | copy-start | bytes 36868
  1759.5 18.4 %copy-start.35 = (f32[512,64]{0,1:T(8,128)S(1)}, f32[512,64]{0,1:T(8,128)}, u32[]{:S(2)}) copy-start(f32[512,64]{0,1:T(8,128)} %param.28) | copy-start | bytes 393220
  1759.5 18.5 %copy-start.37 = (f32[64]{0:T(128)S(1)}, f32[64]{0:T(128)}, u32[]{:S(2)}) copy-start(f32[64]{0:T(128)} %convert_element_type.162) | copy-start | bytes 772
where the time goes:
time: 1790 us; the launch traced here: 1780 us
  matrix products  845 us (47%)
  waiting for transfers between devices  411 us (23%)
  other arithmetic  319 us (18%)
  local copies, waits for them, and re-layouts  164 us (9%)
  starting transfers between devices  39 us (2%)
    dot_general x17, matrix products, per_block(): jnp.einsum('qhd,khd->hqk', q_block, k_all, preferred_element_type=jnp.flo...  244 us
    reduce_sum x17, other arithmetic, per_block(): row_sum = jnp.sum(probs, axis=-1)  219 us
    dot_general x17, matrix products, per_block(): jnp.einsum('hqk,khd->qhd', probs.astype(jnp.bfloat16), v_all, preferred_e...  215 us
    all_to_all x2, waiting for transfers between devices, exchange_attention(): k_all = lax.all_to_all(k_heads, 'sp', 1, 0, tiled=True)  136 us
    all_to_all x2, waiting for transfers between devices, exchange_attention(): q_all = lax.all_to_all(q_heads, 'sp', 1, 0, tiled=True)  121 us
    dot_general x2, matrix products, single_block(): jnp.dot(mlp_act, w_out[d_model:], preferred_element_type=jnp.float32)  105 us
    all_to_all x2, waiting for transfers between devices, exchange_attention(): return lax.all_to_all(attended, 'sp', 0, 1, tiled=True)  93.3 us
    dot_general x1, matrix products, single_block(): jnp.dot(normed, w_in, preferred_element_type=jnp.float32)  89.4 us
  transfers between devices with their start and end apart: 8, of which 7 were waited for; matrix products, arithmetic and copies ran while one was open for 16% of the time, Pallas kernels for 0%

commit v1 on v0

v1 whole, which is shorter than its diff:
```python
import functools
import math

import jax
import jax.numpy as jnp
from jax import lax
from jax.experimental import pallas as pl
from jax.experimental.pallas import tpu as pltpu
from jax.sharding import Mesh, PartitionSpec as P

EPS = 1e-6
LANES = 128
GELU_C = math.sqrt(2.0 / math.pi)
LOG2E = math.log2(math.e)
VMEM_BYTES = 60 * 2**20
PLANE = ('cfg', 'core')


def params(**kw):
    return pltpu.CompilerParams(vmem_limit_bytes=VMEM_BYTES, dimension_semantics=('arbitrary',), **kw)


def ln_mod(x, shift, scale):
    centered = x - jnp.mean(x, axis=-1, keepdims=True)
    var = jnp.mean(centered * centered, axis=-1, keepdims=True)
    return (centered * lax.rsqrt(var + EPS) * (1.0 + scale) + shift).astype(jnp.bfloat16)


def gelu_tanh(u):
    return u * (0.5 * (1.0 + jnp.tanh(GELU_C * (u + 0.044715 * (u * u * u)))))


def mlp_kernel(h_ref, w1_ref, b1_ref, w2_ref, y_ref, u_scr, act, *, row0, n, sub):
    i = pl.program_id(0)
    rows = y_ref.shape[0]
    step = rows // sub

    def up():
        for r in range(sub):
            u = jnp.dot(h_ref[row0 + r * step:row0 + (r + 1) * step, :], w1_ref[0], preferred_element_type=jnp.float32)
            u_scr[r * step:(r + 1) * step, :] = (u + b1_ref[0].astype(jnp.float32)).astype(jnp.bfloat16)

    def gelu():
        act[...] = gelu_tanh(u_scr[...].astype(jnp.float32)).astype(jnp.bfloat16)

    def down(first=False):
        for r in range(sub):
            rs = slice(r * step, (r + 1) * step)
            d = jnp.dot(act[rs, :], w2_ref[0], preferred_element_type=jnp.float32)
            if first:
                y_ref[rs, :] = d
            else:
                y_ref[rs, :] += d

    @pl.when(i == 0)
    def _():
        up()

    @pl.when(i == 1)
    def _():
        gelu()
        up()
        down(True)

    @pl.when((i > 1) & (i < n))
    def _():
        gelu()
        up()
        down()

    @pl.when(i == n)
    def _():
        gelu()
        down()


def mlp(h, w_in, b_in3, w_out, layer, row0, hc=512, sub=2):
    rows, d = h.shape
    ff = w_in.shape[2] - 3 * d
    n = ff // hc
    m = rows - row0
    return pl.pallas_call(
        functools.partial(mlp_kernel, row0=row0, n=n, sub=sub),
        grid=(n + 1,),
        in_specs=[
            pl.BlockSpec((rows, d), lambda i: (0, 0)),
            pl.BlockSpec((1, d, hc), lambda i: (layer, 0, 3 * d // hc + jnp.minimum(i, n - 1))),
            pl.BlockSpec((1, 1, hc), lambda i: (layer, 0, 3 * d // hc + jnp.minimum(i, n - 1))),
            pl.BlockSpec((1, hc, d), lambda i: (layer, d // hc + jnp.maximum(i - 1, 0), 0)),
        ],
        out_specs=pl.BlockSpec((m, d), lambda i: (0, 0)),
        out_shape=jax.ShapeDtypeStruct((m, d), jnp.float32),
        scratch_shapes=[pltpu.VMEM((m, hc), jnp.bfloat16)] * 2,
        compiler_params=params(),
        cost_estimate=pl.CostEstimate(flops=4 * m * d * ff, bytes_accessed=4 * d * ff, transcendentals=m * ff),
        name='mlp',
    )(h, w_in, b_in3, w_out)


def qkv_kernel(head_ref, H_ref, *refs, nh, rb, n_img, n_txt):
    nw = 3 * nh
    w_refs, b_refs = refs[:nw], refs[nw:2 * nw]
    gain_ref, cs_ref, qT_ref, k_ref, vT_ref, wt, bb, gg, hbuf, sem = refs[2 * nw:]
    i = pl.program_id(0)
    n_dev = H_ref.shape[0]
    per = n_img // rb
    n_steps = n_dev * per + 1

    def fetch(step, slot):
        @pl.when(step < n_dev * per)
        def _():
            dev, part = step // per, lax.rem(step, per)
            pltpu.make_async_copy(H_ref.at[dev, pl.ds(n_txt + part * rb, rb), :], hbuf.at[slot], sem.at[slot]).start()

        @pl.when(step == n_dev * per)
        def _():
            for t in range(n_dev):
                pltpu.make_async_copy(H_ref.at[t, pl.ds(0, n_txt), :], hbuf.at[slot, pl.ds(t * n_txt, n_txt), :], sem.at[slot]).start()

    slot = lax.rem(i, 2)

    @pl.when(i == 0)
    def _():
        fetch(0, 0)

    @pl.when(i + 1 < n_steps)
    def _():
        fetch(i + 1, 1 - slot)

    @pl.when(i == 0)
    def _():
        for j in range(nw):
            wt[j * LANES:(j + 1) * LANES, :] = w_refs[j][0].T
            bb[j * LANES:(j + 1) * LANES, :] = jnp.broadcast_to(b_refs[j][0].astype(jnp.float32), (LANES, LANES)).T
        for j in range(2):
            gg[j * LANES:(j + 1) * LANES, :] = jnp.broadcast_to(gain_ref[0, j:j + 1, :].astype(jnp.float32), (LANES, LANES)).T

    pltpu.make_async_copy(H_ref.at[0, pl.ds(0, rb), :], hbuf.at[slot], sem.at[slot]).wait()
    h = hbuf[slot]
    half = LANES // 2
    cos, sin = cs_ref[0:half, :], cs_ref[half:LANES, :]

    def lanes(v):
        return jnp.concatenate([v] * (rb // LANES), axis=1)

    def proj(part):
        rows = slice(part * nh * LANES, (part + 1) * nh * LANES)
        return lax.dot_general(wt[rows, :], h, (((1,), (1,)), ((), ())), preferred_element_type=jnp.float32)

    def bias(x, j):
        return (x + lanes(bb[j * LANES:(j + 1) * LANES, :])).astype(jnp.bfloat16)

    def normed(x, j, g):
        x = bias(x, j).astype(jnp.float32)
        ms = jnp.sum(x * x, axis=0, keepdims=True) * (1.0 / LANES)
        y = x * lax.rsqrt(ms + EPS) * lanes(gg[g * LANES:(g + 1) * LANES, :])
        a, b = y[:half], y[half:]
        return jnp.concatenate([a * cos - b * sin, a * sin + b * cos], axis=0).astype(jnp.bfloat16)

    q = proj(0)
    for t in range(nh):
        qT_ref[t] = normed(q[t * LANES:(t + 1) * LANES], t, 0)
    k = proj(1)
    for t in range(nh):
        k_ref[t] = normed(k[t * LANES:(t + 1) * LANES], nh + t, 1).T
    v = proj(2)
    for t in range(nh):
        vT_ref[t] = bias(v[t * LANES:(t + 1) * LANES], 2 * nh + t)


def qkv(H, head, w_in, b_in3, qk_gain, cs, layer, n_txt, nh):
    n_dev, rows, d = H.shape
    rb = n_dev * n_txt
    n_img = rows - n_txt
    n_heads = d // LANES
    S = n_dev * rows
    stride = n_heads // nh
    steps = n_dev * (n_img // rb) + 1
    blocks = [(p, t) for p in range(3) for t in range(nh)]
    w_specs = [pl.BlockSpec((1, d, LANES), lambda i, r, p=p, t=t: (layer, 0, p * n_heads + t * stride + r[0]), pipeline_mode=pl.Buffered(1)) for p, t in blocks]
    b_specs = [pl.BlockSpec((1, 1, LANES), lambda i, r, p=p, t=t: (layer, 0, p * n_heads + t * stride + r[0])) for p, t in blocks]
    return pl.pallas_call(
        functools.partial(qkv_kernel, nh=nh, rb=rb, n_img=n_img, n_txt=n_txt),
        grid_spec=pltpu.PrefetchScalarGridSpec(
            num_scalar_prefetch=1,
            grid=(steps,),
            in_specs=[pl.BlockSpec(memory_space=pl.ANY)] + w_specs + b_specs + [
                pl.BlockSpec((1, 2, LANES), lambda i, r: (layer, 0, 0)),
                pl.BlockSpec((LANES, rb), lambda i, r: (0, i)),
            ],
            out_specs=[
                pl.BlockSpec((nh, LANES, rb), lambda i, r: (0, 0, i)),
                pl.BlockSpec((nh, rb, LANES), lambda i, r: (0, i, 0)),
                pl.BlockSpec((nh, LANES, rb), lambda i, r: (0, 0, i)),
            ],
            scratch_shapes=[
                pltpu.VMEM((3 * nh * LANES, d), jnp.bfloat16),
                pltpu.VMEM((3 * nh * LANES, LANES), jnp.float32),
                pltpu.VMEM((2 * LANES, LANES), jnp.float32),
                pltpu.VMEM((2, rb, d), jnp.bfloat16),
                pltpu.SemaphoreType.DMA((2,)),
            ],
        ),
        out_shape=[
            jax.ShapeDtypeStruct((nh, LANES, S), jnp.bfloat16),
            jax.ShapeDtypeStruct((nh, S, LANES), jnp.bfloat16),
            jax.ShapeDtypeStruct((nh, LANES, S), jnp.bfloat16),
        ],
        compiler_params=params(),
        cost_estimate=pl.CostEstimate(flops=6 * S * d * nh * LANES, bytes_accessed=2 * S * d + 6 * nh * LANES * d, transcendentals=0),
        name='qkv',
    )(head, H, *([w_in] * (3 * nh)), *([b_in3] * (3 * nh)), qk_gain, cs)


def attn_kernel(qT_ref, k_ref, vT_ref, o_ref, s_scr, m_scr, *, qt, kc, n_img, n_txt, with_txt):
    S, hd = k_ref.shape[1:]
    nk = S // kc
    n_dev = o_ref.shape[0]
    c = hd ** -0.5 * LOG2E
    n_img_tiles = n_dev * n_img // qt
    nq = n_img_tiles + (n_dev * n_txt // qt if with_txt else 0)
    per = n_img // qt

    def score_chunk(q, slot, i, m):
        s = jnp.dot(k_ref[0, pl.ds(i * kc, kc), :], q, preferred_element_type=jnp.float32)
        s_scr[slot, pl.ds(i * kc, kc), :] = s
        return jnp.maximum(m, jnp.max(s.reshape(kc // 8, 8, qt), axis=0))

    def finish_max(m, slot):
        m_scr[slot] = jnp.broadcast_to(jnp.max(m, axis=0, keepdims=True) * c, (8, qt))

    def prob_chunk(mc, slot, i, l, acc):
        s = s_scr[slot, pl.ds(i * kc, kc), :].reshape(kc // 8, 8, qt)
        p = jnp.exp2(s * c - mc[None])
        l = l + jnp.sum(p, axis=0)
        d = jnp.dot(vT_ref[0, :, pl.ds(i * kc, kc)], p.reshape(kc, qt).astype(jnp.bfloat16), preferred_element_type=jnp.float32)
        return l, acc + d

    def emit(t, l, acc, txt):
        o = (acc / jnp.sum(l, axis=0, keepdims=True)).T.astype(o_ref.dtype)
        if txt:
            first = (t - n_img_tiles) * (qt // n_txt)
            for a in range(qt // n_txt):
                o_ref[first + a, 0:n_txt, :] = o[a * n_txt:(a + 1) * n_txt]
        else:
            o_ref[t // per, pl.ds(pl.multiple_of((n_txt if with_txt else 0) + lax.rem(t, per) * qt, 16), qt), :] = o

    def load_q(t):
        return qT_ref[0, :, pl.ds(pl.multiple_of(t * qt, qt), qt)]

    def empty():
        return jnp.zeros((8, qt), jnp.float32), jnp.zeros((hd, qt), jnp.float32)

    def both(t, slot, txt=False):
        q = load_q(t + 1)
        m = jnp.full((8, qt), -jnp.inf, jnp.float32)
        l, acc = empty()
        mc = m_scr[slot]
        for i in range(nk):
            m = score_chunk(q, 1 - slot, i, m)
            l, acc = prob_chunk(mc, slot, i, l, acc)
        finish_max(m, 1 - slot)
        emit(t, l, acc, txt)

    q = load_q(0)
    m = jnp.full((8, qt), -jnp.inf, jnp.float32)
    for i in range(nk):
        m = score_chunk(q, 0, i, m)
    finish_max(m, 0)

    def pair(t2, carry):
        both(2 * t2, 0)
        both(2 * t2 + 1, 1)
        return carry

    pairs = min((nq - 1) // 2, n_img_tiles // 2)
    lax.fori_loop(0, pairs, pair, 0)
    for t in range(2 * pairs, nq - 1):
        both(t, t % 2, t >= n_img_tiles)
    slot = (nq - 1) % 2
    l, acc = empty()
    mc = m_scr[slot]
    for i in range(nk):
        l, acc = prob_chunk(mc, slot, i, l, acc)
    emit(nq - 1, l, acc, nq - 1 >= n_img_tiles)


def largest(n, cap, unit):
    return max(c for c in range(unit, cap + 1, unit) if n % c == 0)


def attention(qT, k, vT, head, n_dev, n_txt, with_txt, qt=256):
    _, S, hd = k.shape
    rows = S // n_dev
    n_img = rows - n_txt
    out_rows = rows if with_txt else n_img
    kc = largest(S, 768, 256)
    SQ = n_dev * out_rows
    return pl.pallas_call(
        functools.partial(attn_kernel, qt=qt, kc=kc, n_img=n_img, n_txt=n_txt, with_txt=with_txt),
        grid=(1,),
        in_specs=[
            pl.BlockSpec((1, hd, S), lambda i: (head, 0, 0)),
            pl.BlockSpec((1, S, hd), lambda i: (head, 0, 0)),
            pl.BlockSpec((1, hd, S), lambda i: (head, 0, 0)),
        ],
        out_specs=pl.BlockSpec((n_dev, out_rows, hd), lambda i: (0, 0, 0)),
        out_shape=jax.ShapeDtypeStruct((n_dev, out_rows, hd), jnp.bfloat16),
        scratch_shapes=[pltpu.VMEM((2, S, qt), jnp.float32), pltpu.VMEM((2, 8, qt), jnp.float32)],
        compiler_params=params(),
        cost_estimate=pl.CostEstimate(flops=6 * SQ * S * hd, bytes_accessed=8 * S * hd, transcendentals=S * SQ),
        name='attn',
    )(qT, k, vT)


def out_kernel(*refs, nh, nc, ne, row0, last):
    o_refs = refs[:nh]
    if last:
        w_ref, bo_ref, mods_ref, wf_ref, bf_ref, x_hbm, y_hbm, vel_ref, lhs, acc, ybuf, xbuf, hs, sems = refs[nh:]
    else:
        w_ref, bo_ref, mods_ref, x_hbm, y_hbm, xo_ref, ho_ref, lhs, acc, ybuf, xbuf, sems = refs[nh:]
    i = pl.program_id(0)
    R = acc.shape[0]
    er = R // ne
    per = nc // nh
    hp = lhs.shape[1] // LANES
    copy_y = pltpu.make_async_copy(y_hbm, ybuf, sems.at[0])
    copy_x = pltpu.make_async_copy(x_hbm.at[pl.ds(row0, R), :], xbuf, sems.at[1])

    @pl.when(i == 0)
    def _():
        copy_y.start()
        copy_x.start()

    for j in range(nh):
        @pl.when((i >= j * per) & (i < (j + 1) * per))
        def _():
            for t in range(hp):
                lhs[:, t * LANES:(t + 1) * LANES] = o_refs[j][t]

    @pl.when(i == 0)
    def _():
        acc[...] = jnp.dot(lhs[...], w_ref[0], preferred_element_type=jnp.float32)

    @pl.when((i > 0) & (i < nc))
    def _():
        acc[...] += jnp.dot(lhs[...], w_ref[0], preferred_element_type=jnp.float32)

    @pl.when(i == nc)
    def _():
        copy_y.wait()
        copy_x.wait()

    @pl.when(i >= nc)
    def _():
        gate, shift, scale = mods_ref[0:1, :], mods_ref[1:2, :], mods_ref[2:3, :]
        bo = bo_ref[0].astype(jnp.float32)
        sub = 16

        def chunk(c, carry):
            rs = pl.ds(pl.multiple_of((i - nc) * er + c * sub, sub), sub)
            ls = pl.ds(pl.multiple_of(c * sub, sub), sub)
            y = acc[rs, :] + ybuf[rs, :] + bo
            xn = (xbuf[rs, :].astype(jnp.float32) + gate * y).astype(jnp.bfloat16)
            h = ln_mod(xn.astype(jnp.float32), shift, scale)
            if last:
                hs[ls, :] = h
            else:
                xo_ref[ls, :] = xn
                ho_ref[ls, :] = h
            return carry

        lax.fori_loop(0, er // sub, chunk, 0, unroll=3 if (er // sub) % 3 == 0 else 2)
        if last:
            vel_ref[...] = jnp.dot(hs[...], wf_ref[...], preferred_element_type=jnp.float32) + bf_ref[...].astype(jnp.float32)


def out_proj(os, w_out, b_out3, mods, x, y_mlp, layer, row0, final=None, kc=512):
    nh = len(os)
    _, R, _ = os[0].shape
    ne = 4 if R % 64 == 0 else 2
    d = w_out.shape[2]
    nc = d // kc
    per = nc // nh
    hp = kc // LANES
    last = final is not None
    in_specs = [pl.BlockSpec((hp, R, LANES), lambda i, j=j: (jnp.clip(i - j * per, 0, per - 1), 0, 0)) for j in range(nh)] + [
        pl.BlockSpec((1, kc, d), lambda i: (layer, jnp.minimum(i, nc - 1), 0)),
        pl.BlockSpec((1, 1, d), lambda i: (layer, 0, 0)),
        pl.BlockSpec((8, d), lambda i: (0, 0)),
    ]
    args = [*os, w_out, b_out3, mods]
    scratch = [pltpu.VMEM((R, kc), jnp.bfloat16), pltpu.VMEM((R, d), jnp.float32), pltpu.VMEM((R, d), jnp.float32), pltpu.VMEM((R, d), jnp.bfloat16)]
    if last:
        n_out = final[0].shape[1]
        in_specs += [pl.BlockSpec((d, n_out), lambda i: (0, 0)), pl.BlockSpec((1, n_out), lambda i: (0, 0))]
        args += list(final)
        out_specs = pl.BlockSpec((R // ne, n_out), lambda i: (jnp.maximum(i - nc, 0), 0))
        out_shape = jax.ShapeDtypeStruct((R, n_out), jnp.float32)
        scratch.append(pltpu.VMEM((R // ne, d), jnp.bfloat16))
    else:
        out_specs = [pl.BlockSpec((R // ne, d), lambda i: (jnp.maximum(i - nc, 0), 0))] * 2
        out_shape = [jax.ShapeDtypeStruct((R, d), jnp.bfloat16)] * 2
    return pl.pallas_call(
        functools.partial(out_kernel, nh=nh, nc=nc, ne=ne, row0=row0, last=last),
        grid=(nc + ne,),
        in_specs=in_specs + [pl.BlockSpec(memory_space=pl.ANY)] * 2,
        out_specs=out_specs,
        out_shape=out_shape,
        scratch_shapes=scratch + [pltpu.SemaphoreType.DMA((2,))],
        compiler_params=params(),
        cost_estimate=pl.CostEstimate(flops=2 * R * d * d, bytes_accessed=2 * d * d + 14 * R * d, transcendentals=0),
        name='outp',
    )(*args, x, y_mlp)


def solution(mesh):
    n_cfg = mesh.devices.shape[0]
    n_core = 2
    n_z = mesh.devices.shape[1] // n_core
    grid = Mesh(mesh.devices.reshape(n_cfg, n_z, n_core), ('cfg', 'z', 'core'))
    assert n_cfg == n_z
    n_dev = n_cfg * n_core
    token_spec = P(('cfg', 'z', 'core'), None)
    seq_spec = P(('z', 'core'), None)
    in_specs = (token_spec, token_spec, P('cfg', None), seq_spec, seq_spec, token_spec) + (P(),) * 13

    def to_plane(v):
        return lax.all_to_all(lax.all_to_all(v, 'cfg', 0, 0), 'z', 0, 0)

    def from_plane(v):
        return lax.all_to_all(lax.all_to_all(v, 'z', 0, 0), 'cfg', 0, 0)

    def body(x_txt, x_img, cond_vec, cos_img, sin_img, z_lat, t_cur, t_next, w_mod, b_mod, w_in, b_in, qk_gain, w_out, b_out, w_fmod, b_fmod, w_final, b_final):
        n_txt, d = x_txt.shape
        n_img = x_img.shape[0]
        n_layers = w_mod.shape[0]
        nh = d // LANES // n_dev
        half = cos_img.shape[1]
        tp, ip = n_txt // n_cfg, n_img // n_cfg
        f32 = jnp.float32

        pieces = to_plane(jnp.concatenate([x_txt.reshape(n_cfg, tp, d), x_img.reshape(n_cfg, ip, d)], axis=1))
        x = jnp.concatenate([pieces[:, :tp].reshape(n_txt, d), pieces[:, tp:].reshape(n_img, d)], axis=0)

        conds = lax.all_gather(cond_vec[0], 'cfg')
        cond = lax.dynamic_slice_in_dim(conds, lax.axis_index('z'), 1, 0)
        s = jax.nn.silu(cond.astype(f32)).astype(jnp.bfloat16)

        def modulation(w, b):
            return (jnp.dot(s, w, preferred_element_type=f32) + b.astype(f32)[None]).reshape(-1, d)

        mods = [modulation(w_mod[l], b_mod[l]) for l in range(n_layers)]
        fmod = modulation(w_fmod, b_fmod)

        tables = jnp.concatenate([cos_img, sin_img], axis=1)
        own = lax.dynamic_slice_in_dim(tables, lax.axis_index('cfg') * ip, ip, 0)
        own = lax.all_gather(own, 'z').reshape(n_img, 2 * half)
        cs = lax.all_gather(own, PLANE).reshape(n_dev * n_img, 2 * half).T
        plain = jnp.concatenate([jnp.ones((half, n_dev * n_txt), f32), jnp.zeros((half, n_dev * n_txt), f32)], axis=0)
        cs = jnp.concatenate([cs, plain], axis=1)

        head = (lax.axis_index('cfg') * n_core + lax.axis_index('core')).astype(jnp.int32).reshape(1)
        b_in3, b_out3 = b_in[:, None, :], b_out[:, None, :]
        x, h = lax.optimization_barrier((x, ln_mod(x.astype(f32), mods[0][0:1], mods[0][1:2])))
        for l in range(n_layers):
            last = l == n_layers - 1
            row0 = n_txt if last else 0
            gathered = lax.all_gather(h, PLANE)
            gathered, y_mlp = lax.optimization_barrier((gathered, mlp(h, w_in, b_in3, w_out, l, row0)))
            qT, k, vT = qkv(gathered, head, w_in, b_in3, qk_gain, cs, l, n_txt, nh)
            os = []
            for t in range(nh):
                o = attention(qT, k, vT, t, n_dev, n_txt, not last)
                os.append(lax.all_to_all(o, PLANE, 0, 0))
            following = fmod if last else mods[l + 1]
            rows = jnp.concatenate([mods[l][2:3], following[0:1], following[1:2], jnp.zeros((5, d), f32)], axis=0)
            if last:
                vel = out_proj(os, w_out, b_out3, rows, x, y_mlp, l, row0, final=(w_final, b_final[None]))
            else:
                x, h = out_proj(os, w_out, b_out3, rows, x, y_mlp, l, row0)

        back = from_plane(vel.reshape(n_z, ip, vel.shape[1])).reshape(n_img, vel.shape[1])
        return z_lat + (t_next - t_cur) * back

    return jax.shard_map(body, mesh=grid, in_specs=in_specs, out_specs=token_spec, check_vma=False)
```

time: 1790 us -> 823 us (0.46)
  matrix products: 845 us -> 55.4 us
  Pallas kernels: 0 us -> 483 us
  other arithmetic: 319 us -> 19.5 us
  waiting for transfers between devices: 411 us -> 138 us
  local copies, waits for them, and re-layouts: 164 us -> 6.7 us
  blocking collectives: 0 us -> 61.9 us
    dot_general x45 -> x3, matrix products: 845 us -> 55.4 us  [modulation(): jnp.dot(s, w, preferred_element_type=f32) + b.astype(f32)[None]]
    pallas_call x0 -> x12, Pallas kernels: none -> 483 us  [the longest x2 201 us: mlp(): pl.pallas_call(functools.partial(mlp_kernel, row0=row0, n=n, sub=sub), gr...]
    all_to_all x8 -> x9, waiting for transfers between devices: 411 us -> 84.1 us  [the longest x2 52.9 us: to_plane(): return lax.all_to_all(lax.all_to_all(v, 'cfg', 0, 0), 'z', 0, 0)]
    reduce_sum x25 -> x2, other arithmetic: 232 us -> 1.62 us  [the longest x1 1.07 us: ln_mod(): var = jnp.mean(centered * centered, axis=-1, keepdims=True)]
    squeeze x1 -> x0, local copies, waits for them, and re-layouts: 85.9 us -> none  [body(): w_in[layer_idx]]
    all_gather x0 -> x3, waiting for transfers between devices: none -> 53.7 us  [the longest x2 53.7 us: body(): gathered = lax.all_gather(h, PLANE)]
    all_gather x0 -> x2, blocking collectives: none -> 51.5 us  [the longest x1 36.4 us: body(): conds = lax.all_gather(cond_vec[0], 'cfg')]
    all_to_all x8 -> x0, local copies, waits for them, and re-layouts: 34 us -> none  [the longest x3 13.8 us: exchange_attention(): return lax.all_to_all(attended, 'sp', 0, 1, tiled=True)]
  transfers between devices with their start and end apart: 8 -> 12, of which waited for: 7 -> 6; matrix products, arithmetic and copies ran while one was open for 16% -> 9% of each run, Pallas kernels for 0% -> 36%
where the time goes in v1:
time: 823 us; the launch traced here: 819 us
  Pallas kernels  483 us (59%)
  waiting for transfers between devices  138 us (17%)
  blocking collectives  61.9 us (8%)
  matrix products  55.4 us (7%)
  starting transfers between devices  39.3 us (5%)
  other arithmetic  19.5 us (2%)
  between operations  15 us (2%)
    pallas_call x2, Pallas kernels, mlp(): pl.pallas_call(functools.partial(mlp_kernel, row0=row0, n=n, sub=sub), gr...  201 us
    pallas_call x6, Pallas kernels, attention(): pl.pallas_call(functools.partial(attn_kernel, qt=qt, kc=kc, n_img=n_img,...  142 us
    pallas_call x2, Pallas kernels, qkv(): pl.pallas_call(functools.partial(qkv_kernel, nh=nh, rb=rb, n_img=n_img, n...  91 us
    dot_general x3, matrix products, modulation(): jnp.dot(s, w, preferred_element_type=f32) + b.astype(f32)[None]  55.4 us
    all_gather x2, waiting for transfers between devices, body(): gathered = lax.all_gather(h, PLANE)  53.7 us
    all_to_all x2, waiting for transfers between devices, to_plane(): return lax.all_to_all(lax.all_to_all(v, 'cfg', 0, 0), 'z', 0, 0)  52.9 us
    pallas_call x2, Pallas kernels, out_proj(): pl.pallas_call(functools.partial(out_kernel, nh=nh, nc=nc, ne=ne, row0=ro...  48.2 us
    all_gather x1, blocking collectives, body(): conds = lax.all_gather(cond_vec[0], 'cfg')  36.4 us
  transfers between devices with their start and end apart: 12, of which 6 were waited for; matrix products, arithmetic and copies ran while one was open for 9% of the time, Pallas kernels for 36%

profile of v1, /device:TPU:0, one launch (start us, length us, event | category | flops | bytes accessed | tf_op | source)
XLA Modules:
  0.0 818.6 jit_solution(13355204022676547126)
XLA Ops:
  6.5 4.0 pad_maximum_fusion
  10.5 5.2 all-to-all-start
  15.8 15.1 %all-gather.1 = f32[512,128]{0,1:T(8,128)} all-gather(f32[128,128]{0,1:T(8,128)S(1)} %fusion.12), channel_id=3, replica_groups=mesh['cfg'=4,'z'=4,'core'=2] {'z'}, dimensions={0}, use_global_device_ids=true | all-gather | bytes 327680 | tf_op jit(solution)/shard_map/all_gather | solution.py:458
  30.9 0.0 all-gather.13.cloned.1.call-update
  30.9 36.4 %all-gather.4 = bf16[4,1,3072]{2,1,0:T(2,128)(2,1)S(1)} all-gather(bf16[1,1,3072]{2,1,0:T(2,128)(2,1)S(1)} %bitcast.81), channel_id=1, replica_groups=mesh['cfg'=4,'z'=4,'core'=2] {'cfg'}, dimensions={0}, use_global_device_ids=true | all-gather | bytes 30720 | tf_op jit(solution)/shard_map/all_gather | solution.py:446
  67.3 20.5 %fusion.2 = f32[1,9216]{1,0:T(1,128)} fusion(bf16[2,3072,9216]{2,1,0:T(8,128)(2,1)} %param.27, bf16[4,1,3072]{2,1,0:T(2,128)(2,1)S(1)} %all-gather.4, s32[]{:T(128)S(6)} %select_n.6), kind=kOutput, calls=%fused_computation.2 | convolution fusion | flops 56641536 | bytes 56672260 | tf_op jit(solution)/shard_map/dot_general | solution.py:451
  87.9 0.0 all-to-all-done
  87.9 5.8 all-to-all-start.1
  93.7 0.3 all-gather.9.cloned.1.call-start
  94.0 20.5 %fusion = f32[1,9216]{1,0:T(1,128)} fusion(bf16[2,3072,9216]{2,1,0:T(8,128)(2,1)} %param.27, bf16[4,1,3072]{2,1,0:T(2,128)(2,1)} %copy-done.8, s32[]{:T(128)S(6)} %select_n.6), kind=kOutput, calls=%fused_computation | convolution fusion | flops 56641536 | bytes 56672260 | tf_op jit(solution)/shard_map/dot_general | solution.py:451
  114.6 0.9 slice_convert_fusion
  115.5 0.8 add.66
  116.3 0.8 add.73
  117.0 0.6 fusion.23
  117.7 52.8 %all-to-all-done.1 = bf16[4,144,3072]{2,1,0:T(8,128)(2,1)S(1)} async-done(((bf16[4,144,3072]{2,1,0:T(8,128)(2,1)}), bf16[4,144,3072]{2,1,0:T(8,128)(2,1)S(1)}, u32[]{:S(2)}, u32[]{:S(2)}) %all-to-all-start.1) | async-done | bytes 3538976 | tf_op jit(solution)/shard_map/all_to_all | solution.py:429
  170.5 0.3 slice.65
  170.9 0.6 convert_reduce_fusion
  171.4 1.1 fusion.8
  172.5 2.0 pad_maximum_fusion.1.refs_6_
  174.5 3.6 fusion.11.h_ref
  178.1 0.0 all-gather.9.cloned.1.call-update
  178.1 0.8 copy.70.b1_ref.refs_9_.refs_10_.refs_11_.refs_12_.refs_13_.refs_14_.refs_15_.refs_16_.refs_17_
  178.9 0.6 copy.80.refs_4_
  179.5 0.6 pad.7.clone
  180.2 14.3 %fusion.13 = f32[1,6144]{1,0:T(1,128)S(1)} fusion(bf16[3072,6144]{1,0:T(8,128)(2,1)} %param.34, bf16[4,1,3072]{2,1,0:T(2,128)(2,1)} %copy-done.8, s32[]{:T(128)S(6)} %select_n.6), kind=kOutput, calls=%fused_computation.29 | convolution fusion | flops 37767168 | bytes 37785604 | tf_op jit(solution)/shard_map/dot_general | solution.py:451
  194.5 0.6 convert_add_fusion
  195.1 3.2 pad_maximum_fusion.2.refs_19_
  198.3 106.4 %mlp.2.refs_7_ = f32[576,3072]{1,0:T(8,128)} custom-call(bf16[576,3072]{1,0:T(8,128)(2,1)} %fusion.11.h_ref, bf16[2,3072,21504]{2,1,0:T(8,128)(2,1)} %refs_8_.3, bf16[2,1,21504]{2,1,0:T(2,128)(2,1)} %copy.70.b1_ref.refs_9_.refs_10_.refs_11_.refs_12_.refs_13_.refs_14_.refs_15_.refs_16_.refs_17_, bf16[2,15360,3072]{2,1,0:T(8,128)(2,1)} %refs_3_.7), custom_call_target="tpu_custom_call" | custom-call | flops 86973087744 | bytes 150994944 | tf_op jit(solution)/shard_map/mlp/pallas_call | solution.py:82
  304.7 9.9 %all-gather.9.cloned.1.call-done = bf16[4608,3072]{1,0:T(8,128)(2,1)} async-done(((bf16[576,3072]{1,0:T(8,128)(2,1)}), bf16[4608,3072]{1,0:T(8,128)(2,1)}) %all-gather.9.cloned.1.call-update) | async-done | bytes 28311568 | tf_op jit(solution)/shard_map/all_gather | solution.py:469
  314.7 45.6 %qkv.2 = (bf16[3,128,4608]{2,1,0:T(8,128)(2,1)}, bf16[3,4608,128]{2,1,0:T(8,128)(2,1)}, bf16[3,128,4608]{2,1,0:T(8,128)(2,1)}) custom-call(s32[1]{0:T(128)} %bitcast.1.head_ref, bf16[8,576,3072]{2,1,0:T(8,128)(2,1)} %bitcast.59, bf16[2,3072,21504]{2,1,0:T(8,128)(2,1)} %refs_8_.3, bf16[2,3072,21504]{2,1,0:T(8,128)(2,1)} %refs_8_.3, ...), custom_call_target="tpu_custom_call" | custom-call | flops 32614907904 | bytes 35389440 | tf_op jit(solution)/shard_map/qkv/pallas_call | solution.py:182
  360.3 25.0 %attn.8 = bf16[8,576,128]{2,1,0:T(8,128)(2,1)} custom-call(bf16[3,128,4608]{2,1,0:T(8,128)(2,1)} %get-tuple-element.21.qT_ref, bf16[3,4608,128]{2,1,0:T(8,128)(2,1)} %get-tuple-element.22.k_ref, bf16[3,128,4608]{2,1,0:T(8,128)(2,1)} %get-tuple-element.23.vT_ref), custom_call_target="tpu_custom_call" | custom-call | flops 16307453952 | bytes 4718592 | tf_op jit(solution)/shard_map/attn/pallas_call | solution.py:299
  385.2 3.8 all-to-all-start.4
  389.0 24.9 %attn.7 = bf16[8,576,128]{2,1,0:T(8,128)(2,1)} custom-call(bf16[3,128,4608]{2,1,0:T(8,128)(2,1)} %get-tuple-element.21.qT_ref, bf16[3,4608,128]{2,1,0:T(8,128)(2,1)} %get-tuple-element.22.k_ref, bf16[3,128,4608]{2,1,0:T(8,128)(2,1)} %get-tuple-element.23.vT_ref), custom_call_target="tpu_custom_call" | custom-call | flops 16307453952 | bytes 4718592 | tf_op jit(solution)/shard_map/attn/pallas_call | solution.py:299
  413.9 0.0 all-to-all-done.4.refs_2_
  413.9 4.2 all-to-all-start.3
  418.2 25.0 %attn.6 = bf16[8,576,128]{2,1,0:T(8,128)(2,1)} custom-call(bf16[3,128,4608]{2,1,0:T(8,128)(2,1)} %get-tuple-element.21.qT_ref, bf16[3,4608,128]{2,1,0:T(8,128)(2,1)} %get-tuple-element.22.k_ref, bf16[3,128,4608]{2,1,0:T(8,128)(2,1)} %get-tuple-element.23.vT_ref), custom_call_target="tpu_custom_call" | custom-call | flops 16307453952 | bytes 4718592 | tf_op jit(solution)/shard_map/attn/pallas_call | solution.py:299
  443.1 0.0 all-to-all-done.3.refs_1_
  443.1 4.2 all-to-all-start.2
  447.3 0.0 all-gather.11.cloned.1.call-start
  447.5 0.8 maximum_maximum_fusion.1
  448.2 14.8 %all-to-all-done.2.refs_0_ = bf16[8,576,128]{2,1,0:T(8,128)(2,1)S(1)} async-done(((bf16[8,576,128]{2,1,0:T(8,128)(2,1)}), bf16[8,576,128]{2,1,0:T(8,128)(2,1)S(1)}, u32[]{:S(2)}, u32[]{:S(2)}) %all-to-all-start.2) | async-done | bytes 1179680 | tf_op jit(solution)/shard_map/all_to_all | solution.py:475
  463.0 1.0 copy-done.2
  464.0 24.0 %outp.2 = (bf16[576,3072]{1,0:T(8,128)(2,1)}, bf16[576,3072]{1,0:T(8,128)(2,1)}) custom-call(bf16[8,576,128]{2,1,0:T(8,128)(2,1)} %copy-done.2, bf16[8,576,128]{2,1,0:T(8,128)(2,1)} %copy-done.1, bf16[8,576,128]{2,1,0:T(8,128)(2,1)} %copy-done, bf16[2,15360,3072]{2,1,0:T(8,128)(2,1)} %refs_3_.7, bf16[2,1,3072]{2,1,0:T(2,128)(2,1)} %copy.80.refs_4_, ...), custom_call_target="tpu_custom_call" | custom-call | flops 10871635968 | bytes 43646976 | tf_op jit(solution)/shard_map/outp/pallas_call | solution.py:404
  488.0 0.0 all-gather.11.cloned.1.call-update
  488.0 94.9 %mlp.3.refs_9_ = f32[512,3072]{1,0:T(8,128)} custom-call(bf16[576,3072]{1,0:T(8,128)(2,1)} %get-tuple-element.26.h_ref, bf16[2,3072,21504]{2,1,0:T(8,128)(2,1)} %refs_8_.3, bf16[2,1,21504]{2,1,0:T(2,128)(2,1)} %copy.70.b1_ref.refs_9_.refs_10_.refs_11_.refs_12_.refs_13_.refs_14_.refs_15_.refs_16_.refs_17_, bf16[2,15360,3072]{2,1,0:T(8,128)(2,1)} %refs_3_.7), custom_call_target="tpu_custom_call" | custom-call | flops 77309411328 | bytes 150994944 | tf_op jit(solution)/shard_map/mlp/pallas_call | solution.py:82
  583.0 43.7 %all-gather.11.cloned.1.call-done = bf16[4608,3072]{1,0:T(8,128)(2,1)} async-done(((bf16[576,3072]{1,0:T(8,128)(2,1)}), bf16[4608,3072]{1,0:T(8,128)(2,1)}) %all-gather.11.cloned.1.call-update) | async-done | bytes 28311568 | tf_op jit(solution)/shard_map/all_gather | solution.py:469
  626.7 45.4 %qkv.3 = (bf16[3,128,4608]{2,1,0:T(8,128)(2,1)}, bf16[3,4608,128]{2,1,0:T(8,128)(2,1)}, bf16[3,128,4608]{2,1,0:T(8,128)(2,1)}) custom-call(s32[1]{0:T(128)} %bitcast.1.head_ref, bf16[8,576,3072]{2,1,0:T(8,128)(2,1)} %bitcast.60, bf16[2,3072,21504]{2,1,0:T(8,128)(2,1)} %refs_8_.3, bf16[2,3072,21504]{2,1,0:T(8,128)(2,1)} %refs_8_.3, ...), custom_call_target="tpu_custom_call" | custom-call | flops 32614907904 | bytes 35389440 | tf_op jit(solution)/shard_map/qkv/pallas_call | solution.py:182
  672.1 22.5 %attn.11 = bf16[8,512,128]{2,1,0:T(8,128)(2,1)} custom-call(bf16[3,128,4608]{2,1,0:T(8,128)(2,1)} %get-tuple-element.28.qT_ref, bf16[3,4608,128]{2,1,0:T(8,128)(2,1)} %get-tuple-element.29.k_ref, bf16[3,128,4608]{2,1,0:T(8,128)(2,1)} %get-tuple-element.30.vT_ref), custom_call_target="tpu_custom_call" | custom-call | flops 14495514624 | bytes 4718592 | tf_op jit(solution)/shard_map/attn/pallas_call | solution.py:299
  694.6 3.8 all-to-all-start.7
  698.4 22.5 %attn.10 = bf16[8,512,128]{2,1,0:T(8,128)(2,1)} custom-call(bf16[3,128,4608]{2,1,0:T(8,128)(2,1)} %get-tuple-element.28.qT_ref, bf16[3,4608,128]{2,1,0:T(8,128)(2,1)} %get-tuple-element.29.k_ref, bf16[3,128,4608]{2,1,0:T(8,128)(2,1)} %get-tuple-element.30.vT_ref), custom_call_target="tpu_custom_call" | custom-call | flops 14495514624 | bytes 4718592 | tf_op jit(solution)/shard_map/attn/pallas_call | solution.py:299
  720.9 0.0 all-to-all-done.7.refs_2_
  720.9 4.2 all-to-all-start.6
  725.1 22.6 %attn.9 = bf16[8,512,128]{2,1,0:T(8,128)(2,1)} custom-call(bf16[3,128,4608]{2,1,0:T(8,128)(2,1)} %get-tuple-element.28.qT_ref, bf16[3,4608,128]{2,1,0:T(8,128)(2,1)} %get-tuple-element.29.k_ref, bf16[3,128,4608]{2,1,0:T(8,128)(2,1)} %get-tuple-element.30.vT_ref), custom_call_target="tpu_custom_call" | custom-call | flops 14495514624 | bytes 4718592 | tf_op jit(solution)/shard_map/attn/pallas_call | solution.py:299
  747.6 0.0 all-to-all-done.6.refs_1_
  747.6 4.5 all-to-all-start.5
  752.2 1.2 copy.92.refs_6_
  753.3 13.0 %all-to-all-done.5.refs_0_ = bf16[8,512,128]{2,1,0:T(8,128)(2,1)S(1)} async-done(((bf16[8,512,128]{2,1,0:T(8,128)(2,1)}), bf16[8,512,128]{2,1,0:T(8,128)(2,1)S(1)}, u32[]{:S(2)}, u32[]{:S(2)}) %all-to-all-start.5) | async-done | bytes 1048608 | tf_op jit(solution)/shard_map/all_to_all | solution.py:475
  766.3 1.0 copy-done.5
  767.3 24.2 %outp.3 = f32[512,64]{1,0:T(8,128)} custom-call(bf16[8,512,128]{2,1,0:T(8,128)(2,1)} %copy-done.5, bf16[8,512,128]{2,1,0:T(8,128)(2,1)} %copy-done.4, bf16[8,512,128]{2,1,0:T(8,128)(2,1)} %copy-done.3, bf16[2,15360,3072]{2,1,0:T(8,128)(2,1)} %refs_3_.7, bf16[2,1,3072]{2,1,0:T(2,128)(2,1)} %copy.80.refs_4_, f32[8,3072]{1,0:T(8,128)} %get-tuple-element.43.refs_5_, ...), custom_call_target="tpu_custom_call" | custom-call | flops 9663676416 | bytes 40894464 | tf_op jit(solution)/shard_map/outp/pallas_call | solution.py:404
  791.5 1.1 copy.93
  792.6 10.4 %all_to_all.50 = f32[4,128,64]{1,2,0:T(8,128)} all-to-all(f32[4,128,64]{1,2,0:T(8,128)S(1)} %copy.93), channel_id=1, replica_groups=mesh['cfg'=4,'z'=4,'core'=2] {'z'}, dimensions={0} | all-to-all | bytes 262144 | tf_op jit(solution)/shard_map/all_to_all | solution.py:432
  803.0 3.3 all-to-all-start.9
  807.6 3.5 all-to-all-done.9
  811.1 0.7 bitcast_add_fusion
  (52 shorter events, 0.2 us)
Async XLA Ops:
  6.5 9.2 %copy-start.9 = (f32[512,64]{0,1:T(8,128)S(1)}, f32[512,64]{0,1:T(8,128)}, u32[]{:S(2)}) copy-start(f32[512,64]{0,1:T(8,128)} %param.22) | copy-start | bytes 393220
  6.5 9.2 %copy-start.10 = (f32[512,64]{0,1:T(8,128)S(1)}, f32[512,64]{0,1:T(8,128)}, u32[]{:S(2)}) copy-start(f32[512,64]{0,1:T(8,128)} %param.23) | copy-start | bytes 393220
  6.5 24.4 %copy-start.20 = (bf16[1,3072]{1,0:T(2,128)(2,1)S(1)}, bf16[1,3072]{1,0:T(2,128)(2,1)}, u32[]{:S(2)}) copy-start(bf16[1,3072]{1,0:T(2,128)(2,1)} %param.21) | copy-start | bytes 18436
  10.5 77.3 %all-to-all-start = ((bf16[4,144,3072]{2,1,0:T(8,128)(2,1)}), bf16[4,144,3072]{2,1,0:T(8,128)(2,1)}, u32[]{:S(2)}, u32[]{:S(2)}) async-start(bf16[4,144,3072]{2,1,0:T(8,128)(2,1)} %pad_maximum_fusion), calls=%async_computation | async-start | bytes 7077888 | tf_op jit(solution)/shard_map/all_to_all | solution.py:429
  15.8 179.4 %all-gather.13.cloned.1.call-start = ((), (), s32[]{:S(2)}) async-start(), calls=%async_computation.12 | async-start | bytes 2359296 | tf_op jit(solution)/shard_map/all_gather | solution.py:459
  67.3 20.5 %copy-start.8 = (bf16[4,1,3072]{2,1,0:T(2,128)(2,1)}, bf16[4,1,3072]{2,1,0:T(2,128)(2,1)S(1)}, u32[]{:S(2)}) copy-start(bf16[4,1,3072]{2,1,0:T(2,128)(2,1)S(1)} %all-gather.4) | copy-start | bytes 73732
  87.9 82.6 %all-to-all-start.1 = ((bf16[4,144,3072]{2,1,0:T(8,128)(2,1)}), bf16[4,144,3072]{2,1,0:T(8,128)(2,1)S(1)}, u32[]{:S(2)}, u32[]{:S(2)}) async-start(bf16[4,144,3072]{2,1,0:T(8,128)(2,1)} %all-to-all-done), calls=%async_computation.1 | async-start | bytes 7077888 | tf_op jit(solution)/shard_map/all_to_all | solution.py:429
  93.7 221.0 %all-gather.9.cloned.1.call-start = ((), (), s32[]{:S(2)}) async-start(), calls=%async_computation.10 | async-start | bytes 31850496 | tf_op jit(solution)/shard_map/all_gather | solution.py:469
  170.9 3.6 copy-start.14
  174.5 3.6 copy-start.13
  174.5 4.4 copy-start.19
  180.2 14.3 %copy-start.21 = (bf16[6144]{0:T(1024)(128)(2,1)S(1)}, bf16[6144]{0:T(1024)(128)(2,1)}, u32[]{:S(2)}) copy-start(bf16[6144]{0:T(1024)(128)(2,1)} %param.35) | copy-start | bytes 36868
  180.2 15.0 %copy-start.7 = (f32[128,512]{1,0:T(8,128)S(1)}, f32[128,512]{1,0:T(8,128)}, u32[]{:S(2)}) copy-start(f32[128,512]{1,0:T(8,128)} %constant.35.clone.1) | copy-start | bytes 786436
  385.2 28.7 %all-to-all-start.4 = ((bf16[8,576,128]{2,1,0:T(8,128)(2,1)}), bf16[8,576,128]{2,1,0:T(8,128)(2,1)S(1)}, u32[]{:S(2)}, u32[]{:S(2)}) async-start(bf16[8,576,128]{2,1,0:T(8,128)(2,1)} %attn.8), calls=%async_computation.4 | async-start | bytes 2359296 | tf_op jit(solution)/shard_map/all_to_all | solution.py:475
  413.9 29.2 %copy-start = (bf16[8,576,128]{2,1,0:T(8,128)(2,1)}, bf16[8,576,128]{2,1,0:T(8,128)(2,1)S(1)}, u32[]{:S(2)}) copy-start(bf16[8,576,128]{2,1,0:T(8,128)(2,1)S(1)} %all-to-all-done.4.refs_2_) | copy-start | bytes 3538948
  413.9 29.2 %all-to-all-start.3 = ((bf16[8,576,128]{2,1,0:T(8,128)(2,1)}), bf16[8,576,128]{2,1,0:T(8,128)(2,1)S(1)}, u32[]{:S(2)}, u32[]{:S(2)}) async-start(bf16[8,576,128]{2,1,0:T(8,128)(2,1)} %attn.7), calls=%async_computation.3 | async-start | bytes 2359296 | tf_op jit(solution)/shard_map/all_to_all | solution.py:475
  418.1 29.3 %copy-start.12 = (f32[6144]{0:T(1024)S(1)}, f32[6144]{0:T(1024)}, u32[]{:S(2)}) copy-start(f32[6144]{0:T(1024)} %convert_add_fusion) | copy-start | bytes 73732
  418.1 29.3 %copy-start.15 = (f32[1,3072]{1,0:T(1,128)S(1)}, f32[1,3072]{1,0:T(1,128)}, u32[]{:S(2)}) copy-start(f32[1,3072]{1,0:T(1,128)} %get-tuple-element.33) | copy-start | bytes 36868
  418.1 29.3 %copy-start.16 = (f32[1,3072]{1,0:T(1,128)S(1)}, f32[1,3072]{1,0:T(1,128)}, u32[]{:S(2)}) copy-start(f32[1,3072]{1,0:T(1,128)} %get-tuple-element.34) | copy-start | bytes 36868
  418.1 29.3 %copy-start.17 = (f32[1,3072]{1,0:T(1,128)S(1)}, f32[1,3072]{1,0:T(1,128)}, u32[]{:S(2)}) copy-start(f32[1,3072]{1,0:T(1,128)} %get-tuple-element.35) | copy-start | bytes 36868
  418.1 29.3 %copy-start.18 = (f32[1,3072]{1,0:T(1,128)S(1)}, f32[1,3072]{1,0:T(1,128)}, u32[]{:S(2)}) copy-start(f32[1,3072]{1,0:T(1,128)} %get-tuple-element.47) | copy-start | bytes 36868
  418.1 29.3 %copy-start.22 = (f32[8]{0:T(128)S(1)}, f32[8]{0:T(128)}, u32[]{:S(2)}) copy-start(f32[8]{0:T(128)} %pad.7.clone) | copy-start | bytes 100
  443.1 19.9 %copy-start.1 = (bf16[8,576,128]{2,1,0:T(8,128)(2,1)}, bf16[8,576,128]{2,1,0:T(8,128)(2,1)S(1)}, u32[]{:S(2)}) copy-start(bf16[8,576,128]{2,1,0:T(8,128)(2,1)S(1)} %all-to-all-done.3.refs_1_) | copy-start | bytes 3538948
  443.1 19.8 %all-to-all-start.2 = ((bf16[8,576,128]{2,1,0:T(8,128)(2,1)}), bf16[8,576,128]{2,1,0:T(8,128)(2,1)S(1)}, u32[]{:S(2)}, u32[]{:S(2)}) async-start(bf16[8,576,128]{2,1,0:T(8,128)(2,1)} %attn.6), calls=%async_computation.2 | async-start | bytes 2359296 | tf_op jit(solution)/shard_map/all_to_all | solution.py:475
  447.3 179.4 %all-gather.11.cloned.1.call-start = ((), (), s32[]{:S(2)}) async-start(), calls=%async_computation.11 | async-start | bytes 31850496 | tf_op jit(solution)/shard_map/all_gather | solution.py:469
  463.0 1.0 copy-start.2
  694.6 26.3 %all-to-all-start.7 = ((bf16[8,512,128]{2,1,0:T(8,128)(2,1)}), bf16[8,512,128]{2,1,0:T(8,128)(2,1)S(1)}, u32[]{:S(2)}, u32[]{:S(2)}) async-start(bf16[8,512,128]{2,1,0:T(8,128)(2,1)} %attn.11), calls=%async_computation.7 | async-start | bytes 2097152 | tf_op jit(solution)/shard_map/all_to_all | solution.py:475
  720.9 26.7 %copy-start.3 = (bf16[8,512,128]{2,1,0:T(8,128)(2,1)}, bf16[8,512,128]{2,1,0:T(8,128)(2,1)S(1)}, u32[]{:S(2)}) copy-start(bf16[8,512,128]{2,1,0:T(8,128)(2,1)S(1)} %all-to-all-done.7.refs_2_) | copy-start | bytes 3145732
  720.9 26.7 %all-to-all-start.6 = ((bf16[8,512,128]{2,1,0:T(8,128)(2,1)}), bf16[8,512,128]{2,1,0:T(8,128)(2,1)S(1)}, u32[]{:S(2)}, u32[]{:S(2)}) async-start(bf16[8,512,128]{2,1,0:T(8,128)(2,1)} %attn.10), calls=%async_computation.6 | async-start | bytes 2097152 | tf_op jit(solution)/shard_map/all_to_all | solution.py:475
  725.1 27.1 %copy-start.6 = (bf16[3072,64]{0,1:T(8,128)(2,1)S(1)}, bf16[3072,64]{0,1:T(8,128)(2,1)}, u32[]{:S(2)}) copy-start(bf16[3072,64]{0,1:T(8,128)(2,1)} %param.36) | copy-start | bytes 1179652
  747.6 18.7 %copy-start.4 = (bf16[8,512,128]{2,1,0:T(8,128)(2,1)}, bf16[8,512,128]{2,1,0:T(8,128)(2,1)S(1)}, u32[]{:S(2)}) copy-start(bf16[8,512,128]{2,1,0:T(8,128)(2,1)S(1)} %all-to-all-done.6.refs_1_) | copy-start | bytes 3145732
  747.6 18.7 %all-to-all-start.5 = ((bf16[8,512,128]{2,1,0:T(8,128)(2,1)}), bf16[8,512,128]{2,1,0:T(8,128)(2,1)S(1)}, u32[]{:S(2)}, u32[]{:S(2)}) async-start(bf16[8,512,128]{2,1,0:T(8,128)(2,1)} %attn.9), calls=%async_computation.5 | async-start | bytes 2097152 | tf_op jit(solution)/shard_map/all_to_all | solution.py:475
  766.3 1.0 copy-start.5
  767.3 43.8 %copy-start.11 = (f32[512,64]{0,1:T(8,128)S(1)}, f32[512,64]{0,1:T(8,128)}, u32[]{:S(2)}) copy-start(f32[512,64]{0,1:T(8,128)} %param.24) | copy-start | bytes 393220
  803.0 8.1 all-to-all-start.9
Sparse Core Ops, SparseCore 0:
  31.1 36.0 all-gather.12
  178.2 136.4 all-gather.8
  488.1 138.5 all-gather.10

commit v2 on v0

v2 whole, which is shorter than its diff:
```python
import functools
import math

import jax
import jax.numpy as jnp
from jax import lax
from jax.experimental import pallas as pl
from jax.experimental.pallas import tpu as pltpu
from jax.sharding import Mesh, PartitionSpec as P

EPS = 1e-6
LANES = 128
GELU_C = math.sqrt(2.0 / math.pi)
LOG2E = math.log2(math.e)
VMEM_BYTES = 60 * 2**20
N_CORE = 2
MESH = pl.DeviceIdType.MESH


def params(**kw):
    return pltpu.CompilerParams(vmem_limit_bytes=VMEM_BYTES, dimension_semantics=('arbitrary',), **kw)


def talking(collective_id):
    return dict(collective_id=collective_id, has_side_effects=True)


def whole(shape, **kw):
    return pl.BlockSpec(shape, lambda i: (0,) * len(shape), **kw)


def head_rows(j):
    return slice(j * LANES, (j + 1) * LANES)


def columns_of(v):
    return jnp.broadcast_to(v.astype(jnp.float32), (LANES, LANES)).T


def wait_for(ref, sem):
    pltpu.make_async_copy(ref, ref, sem).wait()


def dot(a, b):
    return jnp.dot(a, b, preferred_element_type=jnp.float32)


def remote(src, dst, send_sem, recv_sem, device):
    return pltpu.make_async_remote_copy(src_ref=src, dst_ref=dst, send_sem=send_sem, recv_sem=recv_sem, device_id=device, device_id_type=MESH)


def meet(devices):
    barrier = pltpu.get_barrier_semaphore()
    for device in devices:
        pl.semaphore_signal(barrier, inc=1, device_id=device, device_id_type=MESH)
    pl.semaphore_wait(barrier, len(devices))


def ln_mod(x, shift, scale):
    centered = x - jnp.mean(x, axis=-1, keepdims=True)
    var = jnp.mean(centered * centered, axis=-1, keepdims=True)
    return (centered * lax.rsqrt(var + EPS) * (1.0 + scale) + shift).astype(jnp.bfloat16)


def gelu_tanh(u):
    return u * (0.5 * (1.0 + jnp.tanh(GELU_C * (u + 0.044715 * (u * u * u)))))


def related(cfg, core, r):
    cx, cy = cfg // 2, lax.rem(cfg, 2)
    x = lax.rem(cx + lax.rem(r // 2, 2), 2)
    y = lax.rem(cy + r // 4, 2)
    return x * 2 + y, lax.rem(core + lax.rem(r, 2), 2)


def block_kernel(*refs, layer, n, n_dev, nh, n_txt, row0, with_tables, at_x, at_xx):
    h_ref, w1_ref, b1_ref, w2_ref, bias_ref, gain_ref, h_hbm, w_hbm, tab_hbm, y_hbm, H, qT_ref, k_ref, vT_ref, *refs = refs
    T = tab_hbm
    if with_tables:
        T, *refs = refs
    (y_acc, u_scr, act, wt, wbuf, bb, gg, hbuf, tbuf, w_sem, h_sem, y_sem, *refs) = refs
    i = pl.program_id(0)
    cfg, z, core = lax.axis_index('cfg'), lax.axis_index('z'), lax.axis_index('core')
    rows = y_acc.shape[0]
    total, d = h_hbm.shape
    rb = total - n_txt
    half = LANES // 2
    n_heads = d // LANES
    stride = n_heads // nh

    def device(r):
        to, c = related(cfg, core, r)
        return to, z, c

    def slot_of(r):
        to, c = related(cfg, core, r)
        return to * N_CORE + c

    own, X, Y, D = range(0, n_dev, 2)
    A, B = range(2)

    def part_of(ref, piece):
        size = ref.shape[0] // 2
        return ref.at[pl.ds(piece * size, size)]

    arrays = [(h_hbm, H)] + ([(tab_hbm, T)] if with_tables else [])
    if with_tables:
        own_sem, refs = refs[-1], refs[:-1]

    def move(origin, piece, to, send, recv, k_send, k_recv):
        out = []
        for t, (mine, every) in enumerate(arrays):
            dst = part_of(every.at[slot_of(origin)], piece)
            src = part_of(mine, piece) if origin == own else dst
            out.append(remote(src, dst, send[t].at[k_send], recv[t].at[k_recv], device(to)))
        return out

    near_send, near_recv, pair_send, pair_recv = (refs[t::4] for t in range(4))

    def near(origin, piece, to):
        order = 2 if origin else piece
        return move(origin, piece, to, near_send, near_recv, (to - X) // 2 * 3 + order, (origin ^ to) - X + piece)

    def pair(origin, piece):
        return move(origin, piece, 1, pair_send, pair_recv, origin + piece, origin + piece)

    def start(copies):
        for cp in copies:
            cp.start()

    def landed(sems, k, origin, piece):
        for t, (_, every) in enumerate(arrays):
            wait_for(part_of(every.at[slot_of(origin)], piece), sems[t].at[k])

    def landed_near(origin, piece):
        landed(near_recv, origin - X + piece, origin, piece)

    def landed_pair(origin, piece):
        landed(pair_recv, origin + piece, origin + 1, piece)

    def w_copy(j):
        p, t = j // nh, j % nh
        col = (p * n_heads + t * stride + cfg * N_CORE + core) * LANES
        return pltpu.make_async_copy(w_hbm.at[layer, :, pl.ds(pl.multiple_of(col, LANES), LANES)], wbuf.at[j % 2], w_sem.at[j % 2])

    def w_turn(j):
        p, t = j // nh, j % nh
        col = (p * n_heads + t * stride + cfg * N_CORE + core) * LANES
        w_copy(j).wait()
        wt[head_rows(j), :] = wbuf[j % 2].T
        bb[head_rows(j), :] = columns_of(bias_ref[0, :, pl.ds(pl.multiple_of(col, LANES), LANES)])

    def fetch(s, slot):
        @pl.when(s == 0)
        def _():
            pltpu.make_async_copy(h_hbm.at[pl.ds(n_txt, rb), :], hbuf.at[slot], h_sem.at[slot]).start()

        @pl.when((s > 0) & (s < n_dev))
        def _():
            pltpu.make_async_copy(H.at[slot_of(s), pl.ds(n_txt, rb), :], hbuf.at[slot], h_sem.at[slot]).start()

        @pl.when(s == n_dev)
        def _():
            pltpu.make_async_copy(h_hbm.at[pl.ds(0, n_txt), :], hbuf.at[slot, pl.ds(0, n_txt), :], h_sem.at[slot]).start()
            for r in range(1, n_dev):
                pltpu.make_async_copy(H.at[slot_of(r), pl.ds(0, n_txt), :], hbuf.at[slot, pl.ds(r * n_txt, n_txt), :], h_sem.at[slot]).start()

    def fetch_table(s, slot):
        if with_tables:
            @pl.when(s == 0)
            def _():
                pltpu.make_async_copy(tab_hbm, tbuf.at[slot], h_sem.at[2 + slot]).start()

            @pl.when((s > 0) & (s < n_dev))
            def _():
                pltpu.make_async_copy(T.at[slot_of(s)], tbuf.at[slot], h_sem.at[2 + slot]).start()
        else:
            @pl.when(s < n_dev)
            def _():
                pltpu.make_async_copy(T.at[slot_of(s)], tbuf.at[slot], h_sem.at[2 + slot]).start()

    sub = 2
    step = rows // sub

    def up():
        for r in range(sub):
            u = dot(h_ref[row0 + r * step:row0 + (r + 1) * step, :], w1_ref[0])
            u_scr[r * step:(r + 1) * step, :] = (u + b1_ref[0].astype(jnp.float32)).astype(jnp.bfloat16)

    def gelu():
        act[...] = gelu_tanh(u_scr[...].astype(jnp.float32)).astype(jnp.bfloat16)

    def down(first=False):
        for r in range(sub):
            rs = slice(r * step, (r + 1) * step)
            v = dot(act[rs, :], w2_ref[0])
            if first:
                y_acc[rs, :] = v
            else:
                y_acc[rs, :] += v

    @pl.when(i == 0)
    def _():
        w_copy(0).start()
        w_copy(1).start()
        meet([device(1), device(X), device(Y)])
        start(near(own, A, X))
        start(near(own, B, Y))
        start(pair(own, A))
        start(pair(own, B))
        start(near(own, B, X))
        start(near(own, A, Y))
        if with_tables:
            pltpu.make_async_copy(tab_hbm, T.at[slot_of(0)], own_sem).start()
        for j in range(2):
            gg[head_rows(j), :] = columns_of(gain_ref[0, j:j + 1, :])
        up()

    @pl.when(i == 1)
    def _():
        gelu()
        up()
        down(True)

    @pl.when((i > 1) & (i < n))
    def _():
        gelu()
        up()
        down()

    @pl.when(i == n)
    def _():
        gelu()
        down()

    for j in range(3 * nh):
        @pl.when(i == 1 + j)
        def _():
            w_turn(j)
            if j + 2 < 3 * nh:
                w_copy(j + 2).start()

    @pl.when(i == at_x)
    def _():
        landed_near(X, A)
        start(near(X, A, Y))
        start(pair(X, A))
        landed_near(Y, B)
        start(near(Y, B, X))
        start(pair(Y, B))
        landed_pair(own, A)
        landed_pair(own, B)

    @pl.when(i == at_xx)
    def _():
        landed_near(X, B)
        start(pair(X, B))
        landed_near(Y, A)
        start(pair(Y, A))
        landed_pair(X, A)
        landed_pair(Y, B)

    s = i - (n + 1)
    slot = lax.rem(i, 2)

    @pl.when(i == n)
    def _():
        fetch(0, 1 - slot)
        fetch_table(0, 1 - slot)

    @pl.when(s == 0)
    def _():
        pltpu.make_async_copy(y_acc, y_hbm, y_sem).start()
        landed_pair(X, B)
        landed_pair(Y, A)

    @pl.when(s == 2)
    def _():
        landed_near(D, A)
        start(pair(D, A))
        landed_near(D, B)
        start(pair(D, B))

    @pl.when(s == 5)
    def _():
        landed_pair(D, A)
        landed_pair(D, B)

    @pl.when((s >= 0) & (s < n_dev))
    def _():
        fetch(s + 1, 1 - slot)
        fetch_table(s + 1, 1 - slot)

    @pl.when(s >= 0)
    def _():
        pltpu.make_async_copy(h_hbm.at[pl.ds(0, rb), :], hbuf.at[slot], h_sem.at[slot]).wait()

        @pl.when(s < n_dev)
        def _():
            pltpu.make_async_copy(tab_hbm if with_tables else tab_hbm.at[0], tbuf.at[slot], h_sem.at[2 + slot]).wait()
        h = hbuf[slot]
        image = s < n_dev
        table = jnp.concatenate([tbuf[slot, t] for t in range(tbuf.shape[1])], axis=1)
        cos, sin = jnp.where(image, table[:half], 1.0), jnp.where(image, table[half:], 0.0)

        def lanes(v):
            return jnp.concatenate([v] * (rb // LANES), axis=1)

        def proj(part):
            rs = slice(part * nh * LANES, (part + 1) * nh * LANES)
            return lax.dot_general(wt[rs, :], h, (((1,), (1,)), ((), ())), preferred_element_type=jnp.float32)

        def biased(x, j):
            return (x + lanes(bb[head_rows(j), :])).astype(jnp.bfloat16)

        def normed(x, j, g):
            x = biased(x, j).astype(jnp.float32)
            ms = jnp.sum(x * x, axis=0, keepdims=True) * (1.0 / LANES)
            v = x * lax.rsqrt(ms + EPS) * lanes(gg[head_rows(g), :])
            a, b = v[:half], v[half:]
            return jnp.concatenate([a * cos - b * sin, a * sin + b * cos], axis=0).astype(jnp.bfloat16)

        q = proj(0)
        for t in range(nh):
            qT_ref[t] = normed(q[head_rows(t)], t, 0)
        k = proj(1)
        for t in range(nh):
            k_ref[t] = normed(k[head_rows(t)], nh + t, 1).T
        v = proj(2)
        for t in range(nh):
            vT_ref[t] = biased(v[head_rows(t)], 2 * nh + t)

    @pl.when(s == n_dev)
    def _():
        for copies in [near(own, A, X), near(own, B, X), near(own, B, Y), near(own, A, Y), near(Y, B, X), near(X, A, Y)] + [pair(o, p) for o in (own, X, Y, D) for p in (A, B)]:
            for cp in copies:
                cp.wait_send()
        pltpu.make_async_copy(y_acc, y_hbm, y_sem).wait()
        if with_tables:
            pltpu.make_async_copy(tab_hbm, T.at[slot_of(0)], own_sem).wait()


def block(h, w_in, b_in3, w_out, qk_gain, tables, layer, n_txt, nh, row0, collective_id, hc=512):
    total, d = h.shape
    n_dev = d // LANES // nh
    with_tables = tables.ndim == 3
    ff = w_in.shape[2] - 3 * d
    n = ff // hc
    m = total - row0
    rb = total - n_txt
    assert n_dev * n_txt == rb
    S = n_dev * total
    hbm = pl.BlockSpec(memory_space=pl.ANY)
    dma = pltpu.SemaphoreType.DMA
    bf, f32 = jnp.bfloat16, jnp.float32

    def at(i):
        return jnp.clip(i - (n + 1), 0, n_dev)

    t_shape = tables.shape if with_tables else tables.shape[1:]
    out_shape = [jax.ShapeDtypeStruct((m, d), f32), jax.ShapeDtypeStruct((n_dev, total, d), bf),
                 jax.ShapeDtypeStruct((nh, LANES, S), bf), jax.ShapeDtypeStruct((nh, S, LANES), bf), jax.ShapeDtypeStruct((nh, LANES, S), bf)]
    out_specs = [hbm, hbm, pl.BlockSpec((nh, LANES, rb), lambda i: (0, 0, at(i))), pl.BlockSpec((nh, rb, LANES), lambda i: (0, at(i), 0)),
                 pl.BlockSpec((nh, LANES, rb), lambda i: (0, 0, at(i)))]
    sems = [dma((2,)), dma((4,)), dma, dma((6,)), dma((6,)), dma((8,)), dma((8,))]
    if with_tables:
        out_shape.append(jax.ShapeDtypeStruct((n_dev, *tables.shape), f32))
        out_specs.append(hbm)
        sems += [dma((6,)), dma((6,)), dma((8,)), dma((8,)), dma]
    return pl.pallas_call(
        functools.partial(block_kernel, layer=layer, n=n, n_dev=n_dev, nh=nh, n_txt=n_txt, row0=row0, with_tables=with_tables, at_x=n * 5 // 12, at_xx=n * 5 // 6),
        grid=(n + 1 + n_dev + 1,),
        in_specs=[
            whole((total, d), pipeline_mode=pl.Buffered(1)),
            pl.BlockSpec((1, d, hc), lambda i: (layer, 0, 3 * d // hc + jnp.minimum(i, n - 1))),
            pl.BlockSpec((1, 1, hc), lambda i: (layer, 0, 3 * d // hc + jnp.minimum(i, n - 1))),
            pl.BlockSpec((1, hc, d), lambda i: (layer, d // hc + jnp.clip(i - 1, 0, n - 1), 0)),
            pl.BlockSpec((1, 1, b_in3.shape[2]), lambda i: (layer, 0, 0)),
            pl.BlockSpec((1, 2, LANES), lambda i: (layer, 0, 0)),
            hbm, hbm, hbm,
        ],
        out_specs=out_specs,
        out_shape=out_shape,
        scratch_shapes=[
            pltpu.VMEM((m, d), f32), pltpu.VMEM((m, hc), bf), pltpu.VMEM((m, hc), bf), pltpu.VMEM((3 * nh * LANES, d), bf), pltpu.VMEM((2, d, LANES), bf),
            pltpu.VMEM((3 * nh * LANES, LANES), f32), pltpu.VMEM((2 * LANES, LANES), f32), pltpu.VMEM((2, rb, d), bf), pltpu.VMEM((2, *t_shape), f32),
        ] + sems,
        compiler_params=params(**talking(collective_id)),
        cost_estimate=pl.CostEstimate(flops=4 * m * d * ff + 6 * S * d * nh * LANES, bytes_accessed=4 * d * ff + 2 * S * d, transcendentals=m * ff),
        name='block',
    )(h, w_in, b_in3, w_out, b_in3, qk_gain, h, w_in, tables)


def attn_kernel(qT_hbm, k_hbm, vT_hbm, *refs, qt, kc, n_dev, n_img, n_txt, with_txt):
    if with_txt:
        oi_hbm, ot_hbm, qT_ref, k_ref, vT_ref, s_scr, m_scr, obuf, tbuf, in_sem, send_sem, recv_sem, own_sem, tsend_sem, trecv_sem, town_sem = refs
    else:
        oi_hbm, qT_ref, k_ref, vT_ref, s_scr, m_scr, obuf, in_sem, send_sem, recv_sem, own_sem = refs
    nh, S, hd = k_ref.shape
    nk = S // kc
    c = hd ** -0.5 * LOG2E
    per = n_img // qt
    assert per == 2

    def load(t):
        pairs = ((qT_hbm, qT_ref), (k_hbm, k_ref), (vT_hbm, vT_ref))
        return [pltpu.make_async_copy(src.at[t], dst.at[t], in_sem.at[t, j]) for j, (src, dst) in enumerate(pairs)]

    for t in range(nh):
        for cp in load(t):
            cp.start()
    me = lax.axis_index('cfg') * N_CORE + lax.axis_index('core')
    z = lax.axis_index('z')

    def device(r):
        to, c = related(lax.axis_index('cfg'), lax.axis_index('core'), r)
        return to, z, c

    meet([device(r) for r in range(1, n_dev)])
    for cp in load(0):
        cp.wait()

    def score_chunk(head, q, slot, i, m):
        s = dot(k_ref[head, pl.ds(i * kc, kc), :], q)
        s_scr[slot, pl.ds(i * kc, kc), :] = s
        return jnp.maximum(m, jnp.max(s.reshape(kc // 8, 8, qt), axis=0))

    def finish_max(m, slot):
        m_scr[slot] = jnp.broadcast_to(jnp.max(m, axis=0, keepdims=True) * c, (8, qt))

    def prob_chunk(head, mc, slot, i, l, acc):
        s = s_scr[slot, pl.ds(i * kc, kc), :].reshape(kc // 8, 8, qt)
        p = jnp.exp2(s * c - mc[None])
        l = l + jnp.sum(p, axis=0)
        d = dot(vT_ref[head, :, pl.ds(i * kc, kc)], p.reshape(kc, qt).astype(jnp.bfloat16))
        return l, acc + d

    def load_q(tile):
        head, col = tile
        return qT_ref[head, :, pl.ds(pl.multiple_of(col, qt), qt)]

    def start(tile):
        head, _ = tile
        q = load_q(tile)
        m = jnp.full((8, qt), -jnp.inf, jnp.float32)
        for i in range(nk):
            m = score_chunk(head, q, 0, i, m)
        finish_max(m, 0)

    def both(tile, following, slot):
        head, nhead = tile[0], following[0]
        q = load_q(following)
        m = jnp.full((8, qt), -jnp.inf, jnp.float32)
        l = jnp.zeros((8, qt), jnp.float32)
        acc = jnp.zeros((hd, qt), jnp.float32)
        mc = m_scr[slot]
        for i in range(nk):
            m = score_chunk(nhead, q, 1 - slot, i, m)
            l, acc = prob_chunk(head, mc, slot, i, l, acc)
        finish_max(m, 1 - slot)
        return (acc / jnp.sum(l, axis=0, keepdims=True)).T.astype(jnp.bfloat16)

    n_pairs = nh * n_dev

    def relation_of(p):
        return lax.rem(p + 1, n_dev)

    def img_tile(p, part):
        return p // n_dev, relation_of(p) * n_img + part * qt

    def send(p):
        head, owner = p // n_dev, relation_of(p)

        @pl.when(lax.rem(p, n_dev) == n_dev - 1)
        def _():
            pltpu.make_async_copy(obuf.at[p], oi_hbm.at[me, head], own_sem).start()

        @pl.when(lax.rem(p, n_dev) < n_dev - 1)
        def _():
            remote(obuf.at[p], oi_hbm.at[me, head], send_sem, recv_sem, device(owner)).start()

    start(img_tile(0, 0))

    def pair(p, carry):
        @pl.when(p > 0)
        def _():
            send(p - 1)

        @pl.when((lax.rem(p, n_dev) == n_dev - 1) & (p < n_pairs - 1))
        def _():
            for cp in load(p // n_dev + 1):
                cp.wait()

        obuf[p, 0:qt, :] = both(img_tile(p, 0), img_tile(p, 1), 0)
        obuf[p, qt:2 * qt, :] = both(img_tile(p, 1), img_tile(lax.rem(p + 1, n_pairs), 0), 1)
        return carry

    lax.fori_loop(0, n_pairs, pair, 0)
    send(n_pairs - 1)

    if with_txt:
        n_text = n_dev * n_txt
        tiles = n_text // qt
        first = n_dev * n_img

        def txt_tile(u):
            return u // tiles, first + lax.rem(u, tiles) * qt

        def txt_send(u):
            head = u // tiles
            for a in range(qt // n_txt):
                owner = lax.rem(u, tiles) * (qt // n_txt) + a
                src = tbuf.at[u, pl.ds(a * n_txt, n_txt), :]

                @pl.when(owner == 0)
                def _():
                    pltpu.make_async_copy(src, ot_hbm.at[me, head], town_sem).start()

                @pl.when(owner != 0)
                def _():
                    remote(src, ot_hbm.at[me, head], tsend_sem, trecv_sem, device(owner)).start()

        start(txt_tile(0))

        n_tt = nh * tiles
        if n_tt % 2 == 0:
            def txt_pair(p, carry):
                u = 2 * p
                tbuf[u] = both(txt_tile(u), txt_tile(u + 1), 0)
                tbuf[u + 1] = both(txt_tile(u + 1), txt_tile(lax.rem(u + 2, n_tt)), 1)
                txt_send(u)
                txt_send(u + 1)
                return carry
            lax.fori_loop(0, n_tt // 2, txt_pair, 0)
        else:
            for u in range(n_tt):
                tbuf[u] = both(txt_tile(u), txt_tile((u + 1) % n_tt), u % 2)
                txt_send(u)

    others = pl.ds(0, n_dev - 1)
    wait_for(oi_hbm.at[others], send_sem)
    wait_for(oi_hbm.at[others], recv_sem)
    wait_for(oi_hbm.at[me], own_sem)
    if with_txt:
        wait_for(ot_hbm.at[others], tsend_sem)
        wait_for(ot_hbm.at[others], trecv_sem)
        wait_for(ot_hbm.at[me], town_sem)


def largest(n, cap, unit):
    return max(c for c in range(unit, cap + 1, unit) if n % c == 0)


def attention(qT, k, vT, n_dev, n_txt, with_txt, collective_id):
    nh, S, hd = k.shape
    n_img = S // n_dev - n_txt
    qt = n_img // 2
    kc = largest(S, 768, 256)
    SQ = n_dev * (n_img + (n_txt if with_txt else 0))
    dma = pltpu.SemaphoreType.DMA
    out_shape = [jax.ShapeDtypeStruct((n_dev, nh, n_img, hd), jnp.bfloat16)]
    scratch = [pltpu.VMEM((nh, hd, S), jnp.bfloat16), pltpu.VMEM((nh, S, hd), jnp.bfloat16), pltpu.VMEM((nh, hd, S), jnp.bfloat16),
               pltpu.VMEM((2, S, qt), jnp.float32), pltpu.VMEM((2, 8, qt), jnp.float32), pltpu.VMEM((nh * n_dev, n_img, hd), jnp.bfloat16)]
    sems = [dma((nh, 3)), dma, dma, dma]
    if with_txt:
        out_shape.append(jax.ShapeDtypeStruct((n_dev, nh, n_txt, hd), jnp.bfloat16))
        scratch.append(pltpu.VMEM((nh * n_dev * n_txt // qt, qt, hd), jnp.bfloat16))
        sems += [dma, dma, dma]
    return pl.pallas_call(
        functools.partial(attn_kernel, qt=qt, kc=kc, n_dev=n_dev, n_img=n_img, n_txt=n_txt, with_txt=with_txt),
        in_specs=[pl.BlockSpec(memory_space=pl.ANY)] * 3,
        out_specs=[pl.BlockSpec(memory_space=pl.ANY)] * len(out_shape),
        out_shape=out_shape,
        scratch_shapes=scratch + sems,
        compiler_params=pltpu.CompilerParams(vmem_limit_bytes=VMEM_BYTES, **talking(collective_id)),
        cost_estimate=pl.CostEstimate(flops=6 * nh * SQ * S * hd, bytes_accessed=8 * nh * S * hd, transcendentals=nh * S * SQ),
        name='attn',
    )(qT, k, vT)


def out_kernel(*refs, nc, ne, n_txt, row0, last, gate_row):
    if last:
        oi_ref, w_ref, bo_ref, mods_ref, wf_ref, bf_ref, x_hbm, y_hbm, vel_hbm, lhs, acc, ybuf, xbuf, hs, vel, sems, own_sem, send_sem, recv_sem = refs
    else:
        oi_ref, ot_ref, w_ref, bo_ref, mods_ref, x_hbm, y_hbm, xo_ref, ho_ref, lhs, acc, ybuf, xbuf, sems = refs
    i = pl.program_id(0)
    R = acc.shape[0]
    er = R // ne
    copy_y = pltpu.make_async_copy(y_hbm, ybuf, sems.at[0])
    copy_x = pltpu.make_async_copy(x_hbm.at[pl.ds(row0, R), :], xbuf, sems.at[1])

    @pl.when(i == 0)
    def _():
        copy_y.start()
        copy_x.start()

    if last:
        cfg, z, core = lax.axis_index('cfg'), lax.axis_index('z'), lax.axis_index('core')

        @pl.when(i == 0)
        def _():
            meet([(z, e, core) for e in range(ne)] + [(e, cfg, core) for e in range(ne)])

    @pl.when(i < nc)
    def _():
        for t in range(oi_ref.shape[0]):
            cols = head_rows(t)
            if last:
                lhs[:, cols] = oi_ref[t, 0]
            else:
                lhs[:n_txt, cols] = ot_ref[t, 0]
                lhs[n_txt:, cols] = oi_ref[t, 0]

    @pl.when(i == 0)
    def _():
        acc[...] = dot(lhs[...], w_ref[0])

    @pl.when((i > 0) & (i < nc))
    def _():
        acc[...] += dot(lhs[...], w_ref[0])

    @pl.when(i == nc)
    def _():
        copy_y.wait()
        copy_x.wait()

    @pl.when(i >= nc)
    def _():
        gate, shift, scale = (mods_ref[r:r + 1, :] for r in range(gate_row, gate_row + 3))
        bo = bo_ref[0].astype(jnp.float32)
        sub = 16 if er % 16 == 0 else 8

        def chunk(c, carry):
            rs = pl.ds(pl.multiple_of((i - nc) * er + c * sub, sub), sub)
            ls = pl.ds(pl.multiple_of(c * sub, sub), sub)
            y = acc[rs, :] + ybuf[rs, :] + bo
            xn = (xbuf[rs, :].astype(jnp.float32) + gate * y).astype(jnp.bfloat16)
            h = ln_mod(xn.astype(jnp.float32), shift, scale)
            if last:
                hs[ls, :] = h
            else:
                xo_ref[ls, :] = xn
                ho_ref[ls, :] = h
            return carry

        lax.fori_loop(0, er // sub, chunk, 0, unroll=3 if (er // sub) % 3 == 0 else 2)

    if last:
        def deliver(e):
            @pl.when((z == cfg) & (e == z))
            def _():
                pltpu.make_async_copy(vel.at[e], vel_hbm.at[cfg], own_sem).start()

            @pl.when((z != cfg) | (e != z))
            def _():
                remote(vel.at[e], vel_hbm.at[cfg], send_sem.at[e], recv_sem.at[cfg], (z, e, core)).start()

        @pl.when(i >= nc)
        def _():
            vel[i - nc] = dot(hs[...], wf_ref[...]) + bf_ref[...].astype(jnp.float32)
            deliver(i - nc)

        @pl.when(i == nc + ne - 1)
        def _():
            for e in range(ne):
                @pl.when((z == cfg) & (e == z))
                def _():
                    pltpu.make_async_copy(vel.at[e], vel_hbm.at[e], own_sem).wait()

                @pl.when((z != cfg) | (e != z))
                def _():
                    remote(vel.at[e], vel_hbm.at[e], send_sem.at[e], recv_sem.at[e], (z, e, core)).wait_send()
                    remote(vel.at[e], vel_hbm.at[e], send_sem.at[e], recv_sem.at[e], (z, e, core)).wait_recv()


def out_proj(os, w_out, b_out3, mods, x, y_mlp, layer, row0, final=None, collective_id=None, kc=512):
    oi = os[0]
    _, nh, n_img, _ = oi.shape
    R = sum(o.shape[2] for o in os)
    ne = 4
    d = w_out.shape[2]
    nc = d // kc
    per = nc // nh
    hp = kc // LANES
    last = final is not None

    def o_map(i):
        j = jnp.minimum(i, nc - 1)
        return lax.rem(j, per), j // per, 0, 0

    in_specs = [pl.BlockSpec((hp, 1, o.shape[2], LANES), o_map) for o in os] + [
        pl.BlockSpec((1, kc, d), lambda i: (layer, jnp.minimum(i, nc - 1), 0)),
        pl.BlockSpec((1, 1, d), lambda i: (layer, 0, 0)),
        whole(mods.shape),
    ]
    args = [*os, w_out, b_out3, mods]
    scratch = [pltpu.VMEM((R, kc), jnp.bfloat16), pltpu.VMEM((R, d), jnp.float32), pltpu.VMEM((R, d), jnp.float32), pltpu.VMEM((R, d), jnp.bfloat16)]
    sems = [pltpu.SemaphoreType.DMA((2,))]
    if last:
        n_out = final[0].shape[1]
        in_specs += [whole(v.shape) for v in final]
        args += list(final)
        out_specs = pl.BlockSpec(memory_space=pl.ANY)
        out_shape = jax.ShapeDtypeStruct((ne, R // ne, n_out), jnp.float32)
        scratch += [pltpu.VMEM((R // ne, d), jnp.bfloat16), pltpu.VMEM((ne, R // ne, n_out), jnp.float32)]
        sems += [pltpu.SemaphoreType.DMA, pltpu.SemaphoreType.DMA((ne,)), pltpu.SemaphoreType.DMA((ne,))]
        compiler_params = params(**talking(collective_id))
    else:
        out_specs = [pl.BlockSpec((R // ne, d), lambda i: (jnp.maximum(i - nc, 0), 0))] * 2
        out_shape = [jax.ShapeDtypeStruct((R, d), jnp.bfloat16)] * 2
        compiler_params = params()
    return pl.pallas_call(
        functools.partial(out_kernel, nc=nc, ne=ne, n_txt=R - n_img, row0=row0, last=last, gate_row=3 * layer + 2),
        grid=(nc + ne,),
        in_specs=in_specs + [pl.BlockSpec(memory_space=pl.ANY)] * 2,
        out_specs=out_specs,
        out_shape=out_shape,
        scratch_shapes=scratch + sems,
        compiler_params=compiler_params,
        cost_estimate=pl.CostEstimate(flops=2 * R * d * d, bytes_accessed=2 * d * d + 14 * R * d, transcendentals=0),
        name='outp',
    )(*args, x, y_mlp)


def enter_kernel(xt_hbm, xi_hbm, cond_ref, wm_ref, wf_ref, bias_ref, tab_hbm, mods_ref, xo_ref, ho_ref, tab_out,
                 stage, xbuf, cond_buf, s_scr,
                 cond_send, cond_recv, p_send, p_recv, c_send, c_recv, own_sem, t_send, t_recv, town_sem, *, n_mod, n_steps, per_row):
    i = pl.program_id(0)
    n, rows, d = xbuf.shape
    tp = xt_hbm.shape[0] // n
    ip = xi_hbm.shape[0] // n
    cfg, z, core = lax.axis_index('cfg'), lax.axis_index('z'), lax.axis_index('core')
    cx, cy = cfg // 2, lax.rem(cfg, 2)
    across = [(1 - cx) * 2 + cy, cx * 2 + (1 - cy), (1 - cx) * 2 + (1 - cy)]
    heights = [lax.rem(z + s, n) for s in range(1, n)]

    def piece_refs(j, dst):
        return [(xt_hbm.at[pl.ds(j * tp, tp), :], dst.at[pl.ds(0, tp), :]), (xi_hbm.at[pl.ds(j * ip, ip), :], dst.at[pl.ds(tp, ip), :])]

    def forward(group, t):
        @pl.when(group == z)
        def _():
            xbuf[z] = stage[group]

        @pl.when(group != z)
        def _():
            remote(stage.at[group], xbuf.at[z], c_send.at[t], c_recv.at[z], (cfg, group, core)).start()

    @pl.when(i == 0)
    def _():
        meet([(j, z, core) for j in across] + [(cfg, h, core) for h in heights])

        @pl.when(cfg == z)
        def _():
            for t, j in enumerate(across):
                remote(cond_ref, cond_buf, cond_send.at[t], cond_recv, (j, z, core)).start()
        for t, j in enumerate(across):
            for src, dst in piece_refs(j, stage.at[cfg]):
                remote(src, dst, p_send.at[t], p_recv.at[cfg], (j, z, core)).start()

        @pl.when(cfg == z)
        def _():
            for src, dst in piece_refs(cfg, xbuf.at[z]):
                pltpu.make_async_copy(src, dst, own_sem).start()

        @pl.when(cfg != z)
        def _():
            for src, dst in piece_refs(cfg, xbuf.at[z]):
                remote(src, dst, c_send.at[n - 1], c_recv.at[z], (cfg, cfg, core)).start()
        for t, h in enumerate(heights):
            remote(tab_hbm.at[cfg], tab_out.at[z], t_send.at[t], t_recv.at[z], (cfg, h, core)).start()
        pltpu.make_async_copy(tab_hbm.at[cfg], tab_out.at[z], town_sem).start()

        @pl.when(cfg == z)
        def _():
            v = cond_ref[...].astype(jnp.float32)
            s_scr[...] = (v * jax.nn.sigmoid(v)).astype(jnp.bfloat16)

        @pl.when(cfg != z)
        def _():
            remote(cond_ref, cond_buf, cond_send.at[0], cond_recv, (cfg, z, core)).wait_recv()
            v = cond_buf[...].astype(jnp.float32)
            s_scr[...] = (v * jax.nn.sigmoid(v)).astype(jnp.bfloat16)

    row, col = i // per_row, lax.rem(i, per_row)
    width = wm_ref.shape[2]
    cols = pl.ds(pl.multiple_of(col * width, width), width)

    @pl.when(i < n_mod)
    def _():
        v = dot(s_scr[...], wm_ref[0])
        mods_ref[pl.ds(row, 1), cols] = v[0:1]

    @pl.when(i >= n_mod)
    def _():
        v = dot(s_scr[...], wf_ref[...])
        mods_ref[pl.ds(row, 1), cols] = v[0:1]

    def arrived(t):
        j = across[t]
        remote(stage.at[j], stage.at[j], p_send.at[t], p_recv.at[j], (j, z, core)).wait_recv()
        forward(j, t)

    @pl.when(i == n_steps * 3 // 8)
    def _():
        arrived(0)
        arrived(1)

    @pl.when(i == n_steps * 3 // 4)
    def _():
        arrived(2)

    @pl.when(i == n_steps - 1)
    def _():
        mods_ref[...] += bias_ref[...].astype(jnp.float32)
        shift, scale = mods_ref[0:1, :], mods_ref[1:2, :]

        @pl.when(cfg == z)
        def _():
            wait_for(xbuf.at[z], own_sem)

        def norm_rows(k, src, dst, count):
            sub = 16 if count % 16 == 0 else 8

            def chunk(c, carry):
                v = xbuf[k, pl.ds(pl.multiple_of(src + c * sub, sub), sub), :]
                to = pl.ds(pl.multiple_of(dst + c * sub, sub), sub)
                xo_ref[to, :] = v
                ho_ref[to, :] = ln_mod(v.astype(jnp.float32), shift, scale)
                return carry
            lax.fori_loop(0, count // sub, chunk, 0, unroll=min(4, count // sub))

        for s in range(n):
            k = lax.rem(z + s, n)
            if s:
                remote(xbuf.at[k], xbuf.at[k], c_send.at[0], c_recv.at[k], (cfg, k, core)).wait_recv()
            norm_rows(k, 0, k * tp, tp)
            norm_rows(k, tp, n * tp + k * ip, ip)

        for t, j in enumerate(across):
            remote(xbuf.at[0], xbuf.at[0], p_send.at[t], p_recv.at[j], (j, z, core)).wait_send()

            @pl.when(j != z)
            def _():
                remote(xbuf.at[0], xbuf.at[0], c_send.at[t], c_recv.at[j], (cfg, j, core)).wait_send()

        @pl.when(cfg != z)
        def _():
            remote(xbuf.at[0], xbuf.at[0], c_send.at[n - 1], c_recv.at[0], (cfg, cfg, core)).wait_send()

        @pl.when(cfg == z)
        def _():
            for t, j in enumerate(across):
                remote(cond_ref, cond_buf, cond_send.at[t], cond_recv, (j, z, core)).wait_send()
        for t, h in enumerate(heights):
            remote(tab_hbm.at[cfg], tab_out.at[z], t_send.at[t], t_recv.at[z], (cfg, h, core)).wait_send()
            remote(tab_hbm.at[cfg], tab_out.at[h], t_send.at[t], t_recv.at[h], (cfg, h, core)).wait_recv()
        pltpu.make_async_copy(tab_hbm.at[cfg], tab_out.at[z], town_sem).wait()


def enter(x_txt, x_img, cond, w_mod, w_fmod, bias, tables, collective_id, width=512):
    n_txt, d = x_txt.shape
    n_img = x_img.shape[0]
    n = tables.shape[0]
    rows = (n_txt + n_img) // n
    n_layers, _, dm = w_mod.shape
    per_layer, n_fin, per_row = dm // width, w_fmod.shape[1] // width, d // width
    n_mod = n_layers * per_layer
    steps = n_mod + n_fin
    dma = pltpu.SemaphoreType.DMA
    bf = jnp.bfloat16

    def wm_map(i):
        j = jnp.minimum(i, n_mod - 1)
        return j // per_layer, 0, lax.rem(j, per_layer)

    hbm = pl.BlockSpec(memory_space=pl.ANY)
    return pl.pallas_call(
        functools.partial(enter_kernel, n_mod=n_mod, n_steps=steps, per_row=per_row),
        grid=(steps,),
        in_specs=[hbm, hbm, whole(cond.shape), pl.BlockSpec((1, d, width), wm_map), pl.BlockSpec((d, width), lambda i: (0, jnp.maximum(i - n_mod, 0))), whole(bias.shape), hbm],
        out_specs=[whole(bias.shape), whole((n_txt + n_img, d)), whole((n_txt + n_img, d)), hbm],
        out_shape=[jax.ShapeDtypeStruct(bias.shape, jnp.float32), jax.ShapeDtypeStruct((n_txt + n_img, d), bf), jax.ShapeDtypeStruct((n_txt + n_img, d), bf), jax.ShapeDtypeStruct(tables.shape, jnp.float32)],
        scratch_shapes=[pltpu.VMEM((n, rows, d), bf), pltpu.VMEM((n, rows, d), bf), pltpu.VMEM(cond.shape, bf), pltpu.VMEM(cond.shape, bf),
                        dma((n - 1,)), dma, dma((n - 1,)), dma((n,)), dma((n,)), dma((n,)), dma, dma((n - 1,)), dma((n,)), dma],
        compiler_params=params(**talking(collective_id)),
        cost_estimate=pl.CostEstimate(flops=2 * 16 * d * width * steps, bytes_accessed=2 * d * width * steps, transcendentals=0),
        name='enter',
    )(x_txt, x_img, cond, w_mod, w_fmod, bias, tables)


def solution(mesh):
    n_cfg = mesh.devices.shape[0]
    n_z = mesh.devices.shape[1] // N_CORE
    grid = Mesh(mesh.devices.reshape(n_cfg, n_z, N_CORE), ('cfg', 'z', 'core'))
    assert n_cfg == n_z == 4
    n_dev = n_cfg * N_CORE
    token_spec = P(('cfg', 'z', 'core'), None)
    seq_spec = P(('z', 'core'), None)
    in_specs = (token_spec, token_spec, P('cfg', None), seq_spec, seq_spec, token_spec) + (P(),) * 13

    def body(x_txt, x_img, cond_vec, cos_img, sin_img, z_lat, t_cur, t_next, w_mod, b_mod, w_in, b_in, qk_gain, w_out, b_out, w_fmod, b_fmod, w_final, b_final):
        n_txt, d = x_txt.shape
        n_img = x_img.shape[0]
        n_layers = w_mod.shape[0]
        nh = d // LANES // n_dev
        ip = n_img // n_cfg
        n_out = w_final.shape[1]

        tables = jnp.concatenate([cos_img.T, sin_img.T], axis=0).reshape(LANES, n_cfg, ip).transpose(1, 0, 2)
        bias = jnp.concatenate([b_mod.reshape(-1, d), b_fmod.reshape(-1, d)], axis=0)
        cond = jnp.broadcast_to(cond_vec, (16, d))
        mods, x, h, own = enter(x_txt, x_img, cond, w_mod, w_fmod, bias, tables, 1)

        b_in3, b_out3 = b_in[:, None, :], b_out[:, None, :]
        for l in range(n_layers):
            last = l == n_layers - 1
            row0 = n_txt if last else 0
            y_mlp, _, qT, k, vT, *more = block(h, w_in, b_in3, w_out, qk_gain, own, l, n_txt, nh, row0, 2 + 2 * l)
            own = more[0] if more else own
            os = attention(qT, k, vT, n_dev, n_txt, not last, 3 + 2 * l)
            if last:
                wide = [jnp.pad(v, ((0, 0), (0, LANES - n_out))) for v in (w_final, b_final[None])]
                vel = out_proj(os, w_out, b_out3, mods, x, y_mlp, l, row0, final=wide, collective_id=2 + 2 * n_layers)
            else:
                x, h = out_proj(os, w_out, b_out3, mods, x, y_mlp, l, row0)

        return z_lat + (t_next - t_cur) * vel.reshape(n_img, LANES)[:, :n_out]

    return jax.shard_map(body, mesh=grid, in_specs=in_specs, out_specs=token_spec, check_vma=False)
```

time: 1790 us -> 643 us (0.36)
  matrix products: 845 us -> 0 us
  Pallas kernels: 0 us -> 622 us
  waiting for transfers between devices: 411 us -> 0 us
  other arithmetic: 319 us -> 2.2 us
  local copies, waits for them, and re-layouts: 164 us -> 9.53 us
  starting transfers between devices: 39 us -> 0 us
    dot_general x45 -> x0, matrix products: 845 us -> none  [the longest x17 244 us: per_block(): jnp.einsum('qhd,khd->hqk', q_block, k_all, preferred_element_type=jnp.flo...]
    pallas_call x0 -> x7, Pallas kernels: none -> 622 us  [the longest x2 339 us: block(): pl.pallas_call(functools.partial(block_kernel, layer=layer, n=n, n_dev=n_...]
    all_to_all x8 -> x0, waiting for transfers between devices: 411 us -> none  [the longest x2 136 us: exchange_attention(): k_all = lax.all_to_all(k_heads, 'sp', 1, 0, tiled=True)]
    reduce_sum x25 -> x0, other arithmetic: 232 us -> none  [the longest x17 219 us: per_block(): row_sum = jnp.sum(probs, axis=-1)]
    squeeze x1 -> x0, local copies, waits for them, and re-layouts: 85.9 us -> none  [body(): w_in[layer_idx]]
    all_to_all x8 -> x0, starting transfers between devices: 39 us -> none  [the longest x2 11.4 us: exchange_attention(): k_all = lax.all_to_all(k_heads, 'sp', 1, 0, tiled=True)]
    all_to_all x8 -> x0, local copies, waits for them, and re-layouts: 34 us -> none  [the longest x3 13.8 us: exchange_attention(): return lax.all_to_all(attended, 'sp', 0, 1, tiled=True)]
    reshape x3, local copies, waits for them, and re-layouts: 29.9 us -> 2.35 us  [the longest x1 0.84 us: body(): jnp.concatenate([cos_img.T, sin_img.T], axis=0).reshape(LANES, n_cfg, ip)]
  transfers between devices with their start and end apart: 8 -> 0, of which waited for: 7 -> 0; matrix products, arithmetic and copies ran while one was open for 16% -> 0% of each run, Pallas kernels for 0% -> 0%
where the time goes in v2:
time: 643 us; the launch traced here: 635 us
  Pallas kernels  622 us (97%)
  local copies, waits for them, and re-layouts  9.53 us (1%)
    pallas_call x2, Pallas kernels, block(): pl.pallas_call(functools.partial(block_kernel, layer=layer, n=n, n_dev=n_...  339 us
    pallas_call x2, Pallas kernels, attention(): pl.pallas_call(functools.partial(attn_kernel, qt=qt, kc=kc, n_dev=n_dev,...  141 us
    pallas_call x1, Pallas kernels, enter(): pl.pallas_call(functools.partial(enter_kernel, n_mod=n_mod, n_steps=steps...  92.8 us
    pallas_call x2, Pallas kernels, out_proj(): pl.pallas_call(functools.partial(out_kernel, nc=nc, ne=ne, n_txt=R - n_im...  49.5 us

profile of v2, /device:TPU:0, one launch (start us, length us, event | category | flops | bytes accessed | tf_op | source)
XLA Modules:
  0.0 635.1 jit_solution(7541446137165171531)
XLA Ops:
  0.0 1.0 copy.22
  1.0 1.0 copy.23
  2.1 0.1 pad_maximum_fusion
  2.2 0.8 copy.24
  3.1 0.8 reshape.13
  3.9 0.7 reshape.14
  4.6 0.6 pad_maximum_fusion.1.bias_ref
  5.2 0.7 reduce
  6.0 0.7 broadcast_in_dim.18.cond_ref
  6.6 0.0 copy-start.2
  6.6 92.8 %enter.1 = (f32[8,3072]{1,0:T(8,128)}, bf16[576,3072]{1,0:T(8,128)(2,1)}, bf16[576,3072]{1,0:T(8,128)(2,1)}, f32[4,128,128]{2,1,0:T(8,128)}) custom-call(bf16[64,3072]{1,0:T(8,128)(2,1)} %xt_hbm.1, bf16[512,3072]{1,0:T(8,128)(2,1)} %xi_hbm.1, bf16[16,3072]{1,0:T(8,128)(2,1)} %broadcast_in_dim.18.cond_ref, bf16[2,3072,9216]{2,1,0:T(8,128)(2,1)} %wm_ref.1, ...), custom_call_target="tpu_custom_call" | custom-call | flops 2415919104 | bytes 150994944 | tf_op jit(solution)/shard_map/enter/pallas_call | solution.py:878
  99.4 0.0 copy-done.2
  99.4 0.8 copy.25.refs_2_.refs_4_
  100.2 185.3 %block.2 = (f32[576,3072]{1,0:T(8,128)}, bf16[8,576,3072]{2,1,0:T(8,128)(2,1)}, bf16[3,128,4608]{2,1,0:T(8,128)(2,1)}, bf16[3,4608,128]{2,1,0:T(8,128)(2,1)}, bf...) custom-call(bf16[576,3072]{1,0:T(8,128)(2,1)} %get-tuple-element.22.refs_0_.refs_6_, ...), custom_call_target="tpu_custom_call" | custom-call | flops 119587995648 | bytes 179306496 | tf_op jit(solution)/shard_map/block/pallas_call | solution.py:370
  285.4 0.0 copy-start.3
  285.5 78.3 %attn.2 = (bf16[8,3,512,128]{3,2,1,0:T(8,128)(2,1)}, bf16[8,3,64,128]{3,2,1,0:T(8,128)(2,1)}) custom-call(bf16[3,128,4608]{2,1,0:T(8,128)(2,1)} %get-tuple-element.24.qT_hbm, bf16[3,4608,128]{2,1,0:T(8,128)(2,1)} %get-tuple-element.25.k_hbm, bf16[3,128,4608]{2,1,0:T(8,128)(2,1)} %get-tuple-element.26.vT_hbm), custom_call_target="tpu_custom_call" | custom-call | flops 48922361856 | bytes 14155776 | tf_op jit(solution)/shard_map/attn/pallas_call | solution.py:569
  363.8 0.0 copy-done.3
  363.8 0.6 copy.27.refs_3_.refs_2_
  364.5 23.2 %outp.2 = (bf16[576,3072]{1,0:T(8,128)(2,1)}, bf16[576,3072]{1,0:T(8,128)(2,1)}) custom-call(bf16[8,3,512,128]{3,2,1,0:T(8,128)(2,1)} %get-tuple-element.27.refs_0_, bf16[8,3,64,128]{3,2,1,0:T(8,128)(2,1)} %get-tuple-element.28.refs_1_, bf16[2,15360,3072]{2,1,0:T(8,128)(2,1)} %refs_1_.5, bf16[2,1,3072]{2,1,0:T(2,128)(2,1)} %copy.27.refs_3_.refs_2_, ...), custom_call_target="tpu_custom_call" | custom-call | flops 10871635968 | bytes 43646976 | tf_op jit(solution)/shard_map/outp/pallas_call | solution.py:712
  387.7 153.3 %block.3 = (f32[512,3072]{1,0:T(8,128)}, bf16[8,576,3072]{2,1,0:T(8,128)(2,1)}, bf16[3,128,4608]{2,1,0:T(8,128)(2,1)}, bf16[3,4608,128]{2,1,0:T(8,128)(2,1)}, bf16[3,128,4608]{2,1,0:T(8,128)(2,1)}) custom-call(bf16[576,3072]{1,0:T(8,128)(2,1)} %get-tuple-element.32.refs_0_.refs_6_, bf16[2,3072,21504]{2,1,0:T(8,128)(2,1)} %refs_7_.3, ...), custom_call_target="tpu_custom_call" | custom-call | flops 109924319232 | bytes 179306496 | tf_op jit(solution)/shard_map/block/pallas_call | solution.py:370
  540.9 0.0 copy-start
  540.9 0.0 copy-start.4
  541.0 62.5 %attn.3.refs_0_ = bf16[8,3,512,128]{3,2,1,0:T(8,128)(2,1)} custom-call(bf16[3,128,4608]{2,1,0:T(8,128)(2,1)} %get-tuple-element.34.qT_hbm, bf16[3,4608,128]{2,1,0:T(8,128)(2,1)} %get-tuple-element.35.k_hbm, bf16[3,128,4608]{2,1,0:T(8,128)(2,1)} %get-tuple-element.36.vT_hbm), custom_call_target="tpu_custom_call" | custom-call | flops 43486543872 | bytes 14155776 | tf_op jit(solution)/shard_map/attn/pallas_call | solution.py:569
  603.5 0.0 copy-done
  603.5 0.4 copy.30
  603.9 1.1 pad.8.refs_4_
  604.9 0.0 copy-done.4
  604.9 0.5 pad.9.refs_5_
  605.5 0.0 copy-start.1
  605.5 26.3 %outp.3 = f32[4,128,128]{2,1,0:T(8,128)} custom-call(bf16[8,3,512,128]{3,2,1,0:T(8,128)(2,1)} %attn.3.refs_0_, bf16[2,15360,3072]{2,1,0:T(8,128)(2,1)} %refs_1_.5, bf16[2,1,3072]{2,1,0:T(2,128)(2,1)} %copy.27.refs_3_.refs_2_, f32[8,3072]{1,0:T(8,128)} %get-tuple-element.29.refs_4_.refs_3_, bf16[3072,128]{1,0:T(8,128)(2,1)} %pad.8.refs_4_, ...), custom_call_target="tpu_custom_call" | custom-call | flops 9663676416 | bytes 40894464 | tf_op jit(solution)/shard_map/outp/pallas_call | solution.py:712
  631.8 1.1 copy.33
  634.1 0.0 copy-done.1
  634.2 0.7 multiply_add_fusion
Async XLA Ops:
  6.6 92.8 %copy-start.2 = (bf16[2,21504]{1,0:T(2,128)(2,1)S(1)}, bf16[2,21504]{1,0:T(2,128)(2,1)}, u32[]{:S(2)}) copy-start(bf16[2,21504]{1,0:T(2,128)(2,1)} %param.30) | copy-start | bytes 258052
  285.4 78.4 %copy-start.3 = (bf16[2,3072]{1,0:T(2,128)(2,1)S(1)}, bf16[2,3072]{1,0:T(2,128)(2,1)}, u32[]{:S(2)}) copy-start(bf16[2,3072]{1,0:T(2,128)(2,1)} %param.33) | copy-start | bytes 36868
  540.9 62.6 %copy-start = (bf16[3072,64]{0,1:T(8,128)(2,1)S(1)}, bf16[3072,64]{0,1:T(8,128)(2,1)}, u32[]{:S(2)}) copy-start(bf16[3072,64]{0,1:T(8,128)(2,1)} %param.36) | copy-start | bytes 1179652
  540.9 64.0 %copy-start.4 = (bf16[64]{0:T(256)(128)(2,1)S(1)}, bf16[64]{0:T(256)(128)(2,1)}, u32[]{:S(2)}) copy-start(bf16[64]{0:T(256)(128)(2,1)} %param.37) | copy-start | bytes 388
  605.5 28.7 %copy-start.1 = (f32[512,64]{0,1:T(8,128)S(1)}, f32[512,64]{0,1:T(8,128)}, u32[]{:S(2)}) copy-start(f32[512,64]{0,1:T(8,128)} %param.24) | copy-start | bytes 393220
